TPU v7x, 32 devices: a whole 2x2x4 slice. The times are simulated.
32 devices in a mesh: dp: 4 (over y, core), seq: 8 (over z, x).
Axes of the slice: x: 2, y: 2, z: 4, core: 2. Of those that a mesh axis runs over, the one named last changes fastest.
Arguments:
- queries: bfloat16 [32, 2048, 512], P('dp', 'seq'), may hold values from -6 to 6
- enc_keys: bfloat16 [32, 2048, 512], P('dp', 'seq'), may hold values from -6 to 6
- enc_values: bfloat16 [32, 2048, 512], P('dp', 'seq'), may hold values from -6 to 6
- dec_ids: int32 [32, 2048], P('dp', 'seq'), may hold values from 0 to 15, never falling along the last dimension, each value on 1 to 512 neighbouring positions
- enc_ids: int32 [32, 2048], P('dp', 'seq'), may hold values from 0 to 15, never falling along the last dimension, each value on 1 to 512 neighbouring positions
Outputs:
- context: bfloat16 [32, 2048, 512], P('dp', 'seq')
Inputs may be any that keep to these rules, and one draw needn't show every extreme that they name: `dec_ids`: along each row the numbers never fall; every number from 0 to 15 occurs in every row; a document holds 1 to 512 positions of a row, and some document holds exactly 512. `enc_ids`: along each row the numbers never fall; every number from 0 to 15 occurs in every row; a document holds 1 to 512 positions of a row, and some document holds exactly 512.
All inputs are finite; a program needn't handle non-finite values.
Results may differ from a plain program's by a relative error of at most 0.0047.
Values may be sent and summed in bfloat16 or wider, within the bound.
A program may use at most 128 MiB of HBM per device.

v0:
```python
import jax
import jax.numpy as jnp
from jax import lax
from jax.sharding import PartitionSpec as P

HEAD_DIM = 64


masked_score = -1e30


def shortened(value):

    def short(part):
        return part.astype(jnp.bfloat16) if part.dtype == jnp.float32 else part

    return jax.tree.map(short, value)


def attend_dense(query_row, key_row, value_row, dec_row, enc_row, head_count):
    length = query_row.shape[0]
    query_heads = query_row.reshape(length, head_count, HEAD_DIM)
    key_heads = key_row.reshape(length, head_count, HEAD_DIM)
    value_heads = value_row.reshape(length, head_count, HEAD_DIM)
    query_span = min(512, length)
    pieces = []
    for offset in range(0, length, query_span):
        scores = jnp.einsum(
            "qhd,khd->hqk",
            query_heads[offset : offset + query_span],
            key_heads,
            preferred_element_type=jnp.float32,
        )
        allowed = (dec_row[offset : offset + query_span][:, None] == enc_row[None, :])[None]
        scores = jnp.where(allowed, scores, masked_score)
        row_peak = jnp.max(scores, axis=2, keepdims=True)
        expos = jnp.where(allowed, jnp.exp(scores - row_peak), 0.0)
        row_total = jnp.sum(expos, axis=2, keepdims=True)
        weights = (expos / row_total).astype(jnp.bfloat16)
        summed = jnp.einsum(
            "hqk,khd->qhd", weights, value_heads, preferred_element_type=jnp.float32
        )
        pieces.append(summed.reshape(query_span, head_count * HEAD_DIM).astype(jnp.bfloat16))
    return jnp.concatenate(pieces, axis=0)


def local(queries, enc_keys, enc_values, dec_ids, enc_ids):
    group = lax.axis_size("seq")
    dec_spread = jnp.broadcast_to(
        dec_ids.astype(jnp.bfloat16)[:, :, None], (dec_ids.shape[0], dec_ids.shape[1], group)
    )
    enc_spread = jnp.broadcast_to(
        enc_ids.astype(jnp.bfloat16)[:, :, None], (enc_ids.shape[0], enc_ids.shape[1], group)
    )
    members = (
        lax.all_to_all(queries, "seq", split_axis=2, concat_axis=1, tiled=True),
        lax.all_to_all(enc_keys, "seq", split_axis=2, concat_axis=1, tiled=True),
        lax.all_to_all(enc_values, "seq", split_axis=2, concat_axis=1, tiled=True),
        lax.all_to_all(dec_spread, "seq", split_axis=2, concat_axis=1, tiled=True),
        lax.all_to_all(enc_spread, "seq", split_axis=2, concat_axis=1, tiled=True),
    )
    dec_rows = members[3][:, :, 0].astype(jnp.int32)
    enc_rows = members[4][:, :, 0].astype(jnp.int32)
    query_rows = members[0]
    key_rows = members[1]
    value_rows = members[2]
    head_count = query_rows.shape[2] // HEAD_DIM

    def one_row(members):
        return attend_dense(members[0], members[1], members[2], members[3], members[4], head_count)

    attended = lax.map(one_row, (query_rows, key_rows, value_rows, dec_rows, enc_rows))
    return lax.all_to_all(
        shortened(attended), "seq", split_axis=1, concat_axis=2, tiled=True
    ).astype(attended.dtype)


def solution(mesh):
    in_specs = (
        P("dp", "seq", None),
        P("dp", "seq", None),
        P("dp", "seq", None),
        P("dp", "seq"),
        P("dp", "seq"),
    )
    out_specs = P("dp", "seq", None)
    return jax.shard_map(local, mesh=mesh, in_specs=in_specs, out_specs=out_specs, check_vma=False)
```

profile of v0, /device:TPU:0, one launch (start us, length us, event | category | flops | bytes accessed | tf_op | source)
XLA Modules:
  0.0 412.9 jit_solution(16733577638339409978)
XLA Ops:
  1.3 7.3 %all-to-all-start.1 = ((bf16[8,256,8]{1,0,2:T(8,128)(2,1)}), bf16[8,256,8]{1,0,2:T(8,128)(2,1)S(1)}, u32[]{:S(2)}, u32[]{:S(2)}) async-start(bf16[8,256,8]{1,0,2:T(8,128)(2,1)} %broadcast_in_dim.23), calls=%async_computation.1 | async-start | bytes 65536 | tf_op jit(solution)/shard_map/all_to_all | solution.py:59
  9.3 6.0 %all-to-all-done.1 = bf16[8,256,8]{1,0,2:T(8,128)(2,1)S(1)} async-done(((bf16[8,256,8]{1,0,2:T(8,128)(2,1)}), bf16[8,256,8]{1,0,2:T(8,128)(2,1)S(1)}, u32[]{:S(2)}, u32[]{:S(2)}) %all-to-all-start.1) | async-done | bytes 32800 | tf_op jit(solution)/shard_map/all_to_all | solution.py:59
  15.9 3.3 all-to-all-start.2
  19.2 4.5 %copy.25 = bf16[8,256,512]{1,0,2:T(8,128)(2,1)} copy(bf16[8,256,512]{2,1,0:T(8,128)(2,1)} %param.9) | data formatting | bytes 4194304 | tf_op args[2]
  23.7 2.1 all-to-all-done.2
  25.9 3.8 all-to-all-start
  29.7 4.5 %copy.28 = bf16[8,256,512]{1,0,2:T(8,128)(2,1)} copy(bf16[8,256,512]{2,1,0:T(8,128)(2,1)} %param.7) | data formatting | bytes 4194304 | tf_op args[0]
  34.2 42.1 %all-to-all-done = bf16[8,256,512]{1,0,2:T(8,128)(2,1)S(1)} async-done(((bf16[8,256,512]{1,0,2:T(8,128)(2,1)}), bf16[8,256,512]{1,0,2:T(8,128)(2,1)S(1)}, u32[]{:S(2)}, u32[]{:S(2)}) %all-to-all-start) | async-done | bytes 2097184 | tf_op jit(solution)/shard_map/all_to_all | solution.py:58
  76.3 4.4 %all-to-all-start.3 = ((bf16[8,256,512]{1,0,2:T(8,128)(2,1)}), bf16[8,256,512]{1,0,2:T(8,128)(2,1)}, u32[]{:S(2)}, u32[]{:S(2)}) async-start(bf16[8,256,512]{1,0,2:T(8,128)(2,1)} %copy.28), calls=%async_computation.3 | async-start | bytes 4194304 | tf_op jit(solution)/shard_map/all_to_all | solution.py:56
  80.7 4.5 %copy.31 = bf16[8,256,512]{1,0,2:T(8,128)(2,1)} copy(bf16[8,256,512]{2,1,0:T(8,128)(2,1)} %param.8) | data formatting | bytes 4194304 | tf_op args[1]
  85.2 43.1 %all-to-all-done.3 = bf16[8,256,512]{1,0,2:T(8,128)(2,1)} async-done(((bf16[8,256,512]{1,0,2:T(8,128)(2,1)}), bf16[8,256,512]{1,0,2:T(8,128)(2,1)}, u32[]{:S(2)}, u32[]{:S(2)}) %all-to-all-start.3) | async-done | bytes 2097184 | tf_op jit(solution)/shard_map/all_to_all | solution.py:56
  128.3 4.4 %all-to-all-start.4 = ((bf16[8,256,512]{1,0,2:T(8,128)(2,1)}), bf16[8,256,512]{1,0,2:T(8,128)(2,1)}, u32[]{:S(2)}, u32[]{:S(2)}) async-start(bf16[8,256,512]{1,0,2:T(8,128)(2,1)} %copy.31), calls=%async_computation.4 | async-start | bytes 4194304 | tf_op jit(solution)/shard_map/all_to_all | solution.py:57
  132.7 3.5 copy.42
  136.3 5.0 %copy.44 = bf16[8,8,256,64]{3,2,1,0:T(8,128)(2,1)} copy(bf16[8,8,256,64]{2,0,3,1:T(8,128)(2,1)} %bitcast.36) | data formatting | bytes 4194304 | tf_op jit(solution)/shard_map/while | solution.py:72
  141.3 39.2 %all-to-all-done.4 = bf16[8,256,512]{1,0,2:T(8,128)(2,1)} async-done(((bf16[8,256,512]{1,0,2:T(8,128)(2,1)}), bf16[8,256,512]{1,0,2:T(8,128)(2,1)}, u32[]{:S(2)}, u32[]{:S(2)}) %all-to-all-start.4) | async-done | bytes 2097184 | tf_op jit(solution)/shard_map/all_to_all | solution.py:57
  180.5 5.0 %copy.46 = bf16[8,8,256,64]{3,2,1,0:T(8,128)(2,1)} copy(bf16[8,8,256,64]{2,0,3,1:T(8,128)(2,1)} %bitcast.40) | data formatting | bytes 4194304 | tf_op jit(solution)/shard_map/while | solution.py:72
  185.5 150.7 %while.10 = (s32[]{:T(128)}, bf16[8,2048,64]{1,2,0:T(8,128)(2,1)S(1)}, bf16[8,2048,64]{2,1,0:T(8,128)(2,1)}, s32[8,2048]{1,0:T(8,128)S(1)}, s32[8,2048]{1,0:T(8,...) while((s32[]{:T(128)}, ...), condition=%wide.region_9.10_spmd, body=%wide.region_0.9_spmd.sunk | while | flops 1133637632 | bytes 72773864 | solution.py:72
  185.6 2.0 fusion.83
  191.2 3.9 fusion.85
  196.5 3.4 fusion.86
  204.4 2.0 fusion.83
  210.1 3.9 fusion.85
  215.4 3.4 fusion.86
  223.3 2.0 fusion.83
  227.0 1.8 fusion.84
  228.9 3.9 fusion.85
  234.2 3.4 fusion.86
  242.1 2.0 fusion.83
  247.7 3.9 fusion.85
  253.0 3.4 fusion.86
  260.9 2.0 fusion.83
  266.6 3.9 fusion.85
  271.9 3.4 fusion.86
  279.8 2.0 fusion.83
  285.4 3.9 fusion.85
  290.7 3.4 fusion.86
  298.6 2.0 fusion.83
  304.2 3.9 fusion.85
  309.6 3.4 fusion.86
  317.4 2.0 fusion.83
  323.1 3.9 fusion.85
  328.4 3.4 fusion.86
  336.2 4.3 %copy.37 = bf16[8,2048,64]{2,0,1:T(8,128)(2,1)} copy(bf16[8,2048,64]{1,2,0:T(8,128)(2,1)S(1)} %get-tuple-element.42) | data formatting | bytes 4194304 | tf_op jit(solution)/shard_map/while | solution.py:72
  340.5 6.4 %reshape.166 = bf16[8,2,65536]{2,1,0:T(2,128)(2,1)S(1)} reshape(bf16[2048,8,64]{2,1,0:T(8,128)(2,1)} %bitcast.147) | data formatting | bytes 4194304
  346.8 51.8 %all_to_all.90 = bf16[8,2,65536]{2,1,0:T(2,128)(2,1)} all-to-all(bf16[8,2,65536]{2,1,0:T(2,128)(2,1)S(1)} %reshape.166), channel_id=1, replica_groups=mesh['dp'=4,'seq'=8] {'seq'}, dimensions={0} | all-to-all | bytes 4194304 | tf_op jit(solution)/shard_map/all_to_all | solution.py:73
  398.7 7.4 %reshape.167 = bf16[2048,8,64]{2,1,0:T(8,128)(2,1)} reshape(bf16[8,2,65536]{2,1,0:T(2,128)(2,1)} %all_to_all.90) | data formatting | bytes 4194304
  406.1 4.5 %copy.39 = bf16[8,256,8,64]{1,3,2,0:T(8,128)(2,1)S(1)} copy(bf16[8,256,8,64]{3,0,1,2:T(8,128)(2,1)} %bitcast.148) | data formatting | bytes 4194304 | tf_op jit(solution)/shard_map/all_to_all | solution.py:73
  410.5 2.4 copy.40
  (96 shorter events, 77.0 us)
Async XLA Ops:
  1.3 14.0 %all-to-all-start.1 = ((bf16[8,256,8]{1,0,2:T(8,128)(2,1)}), bf16[8,256,8]{1,0,2:T(8,128)(2,1)S(1)}, u32[]{:S(2)}, u32[]{:S(2)}) async-start(bf16[8,256,8]{1,0,2:T(8,128)(2,1)} %broadcast_in_dim.23), calls=%async_computation.1 | async-start | bytes 65536 | tf_op jit(solution)/shard_map/all_to_all | solution.py:59
  15.9 10.0 %all-to-all-start.2 = ((bf16[8,256,8]{1,0,2:T(8,128)(2,1)}), bf16[8,256,8]{1,0,2:T(8,128)(2,1)S(1)}, u32[]{:S(2)}, u32[]{:S(2)}) async-start(bf16[8,256,8]{1,0,2:T(8,128)(2,1)} %broadcast_in_dim.24), calls=%async_computation.2 | async-start | bytes 65536 | tf_op jit(solution)/shard_map/all_to_all | solution.py:60
  25.9 50.4 %all-to-all-start = ((bf16[8,256,512]{1,0,2:T(8,128)(2,1)}), bf16[8,256,512]{1,0,2:T(8,128)(2,1)S(1)}, u32[]{:S(2)}, u32[]{:S(2)}) async-start(bf16[8,256,512]{1,0,2:T(8,128)(2,1)} %copy.25), calls=%async_computation | async-start | bytes 4194304 | tf_op jit(solution)/shard_map/all_to_all | solution.py:58
  76.3 52.0 %all-to-all-start.3 = ((bf16[8,256,512]{1,0,2:T(8,128)(2,1)}), bf16[8,256,512]{1,0,2:T(8,128)(2,1)}, u32[]{:S(2)}, u32[]{:S(2)}) async-start(bf16[8,256,512]{1,0,2:T(8,128)(2,1)} %copy.28), calls=%async_computation.3 | async-start | bytes 4194304 | tf_op jit(solution)/shard_map/all_to_all | solution.py:56
  128.3 52.2 %all-to-all-start.4 = ((bf16[8,256,512]{1,0,2:T(8,128)(2,1)}), bf16[8,256,512]{1,0,2:T(8,128)(2,1)}, u32[]{:S(2)}, u32[]{:S(2)}) async-start(bf16[8,256,512]{1,0,2:T(8,128)(2,1)} %copy.31), calls=%async_computation.4 | async-start | bytes 4194304 | tf_op jit(solution)/shard_map/all_to_all | solution.py:57
  141.3 44.2 %copy-start.1 = (bf16[8,2048,64]{1,2,0:T(8,128)(2,1)S(1)}, bf16[8,2048,64]{1,2,0:T(8,128)(2,1)}, u32[]{:S(2)}) copy-start(bf16[8,2048,64]{1,2,0:T(8,128)(2,1)} %custom-call) | copy-start | bytes 6291460
  191.2 3.9 copy-start
  210.0 3.9 copy-start
  228.9 3.9 copy-start
  247.7 3.9 copy-start
  266.6 3.9 copy-start
  285.4 3.9 copy-start
  304.2 3.9 copy-start
  323.1 3.9 copy-start
where the time goes:
time: 415 us; the launch traced here: 413 us
  waiting for transfers between devices  133 us (32%)
  matrix products  122 us (29%)
  local copies, waits for them, and re-layouts  54 us (13%)
  blocking collectives  51.8 us (12%)
  other arithmetic  29 us (7%)
  starting transfers between devices  23.1 us (6%)
    dot_general x32, matrix products, attend_dense(): jnp.einsum('qhd,khd->hqk', query_heads[offset:offset + query_span], key_h...  75.9 us
    all_to_all x1, blocking collectives, local(): lax.all_to_all(shortened(attended), 'seq', split_axis=1, concat_axis=2, t...  51.8 us
    dot_general x32, matrix products, attend_dense(): jnp.einsum('hqk,khd->qhd', weights, value_heads, preferred_element_type=j...  45.9 us
    all_to_all x1, waiting for transfers between devices, local(): lax.all_to_all(queries, 'seq', split_axis=2, concat_axis=1, tiled=True)  43.1 us
    all_to_all x1, waiting for transfers between devices, local(): lax.all_to_all(enc_values, 'seq', split_axis=2, concat_axis=1, tiled=True)  42.1 us
    all_to_all x1, waiting for transfers between devices, local(): lax.all_to_all(enc_keys, 'seq', split_axis=2, concat_axis=1, tiled=True)  39.2 us
    reduce_sum x8, other arithmetic, attend_dense(): row_total = jnp.sum(expos, axis=2, keepdims=True)  27.4 us
    unnamed x7, local copies, waits for them, and re-layouts  27.3 us
  transfers between devices with their start and end apart: 5, of which 5 were waited for; matrix products, arithmetic and copies ran while one was open for 6% of the time, Pallas kernels for 0%

commit v1 on v0

v1 whole, which is shorter than its diff:
```python
import functools

import jax
import jax.numpy as jnp
from jax import lax
from jax.experimental import pallas as pl
from jax.experimental.pallas import tpu as pltpu
from jax.sharding import PartitionSpec as P

HEAD_DIM = 64
DOCS = 16
CHUNKS = 4
SPAN = 256
MASKED = -8192.0


def pack_kernel(q_ref, k_ref, v_ref, o_ref):
    group, _, _, width, count = o_ref.shape
    for slot, ref in enumerate((q_ref, k_ref, v_ref)):
        o_ref[:, slot, 0] = ref[0].T.reshape(group, width, count)


def pack(q, k, v, group, first, rows):
    _, count, features = q.shape
    width = features // group
    spec = pl.BlockSpec((1, count, features), lambda r: (r + first, 0, 0))
    return pl.pallas_call(
        pack_kernel,
        grid=(rows,),
        in_specs=[spec] * 3,
        out_specs=pl.BlockSpec((group, 3, 1, width, count), lambda r: (0, 0, r, 0, 0)),
        out_shape=jax.ShapeDtypeStruct((group, 3, rows, width, count), q.dtype),
        cost_estimate=pl.CostEstimate(
            flops=4 * rows * count * features, bytes_accessed=12 * rows * count * features, transcendentals=0
        ),
    )(q, k, v)


def unpack_kernel(x_ref, *rest):
    o_ref = rest[-1]
    group, _, width, count = x_ref.shape
    o_ref[0] = x_ref[:, 0].reshape(group * width, count).T


def unpack(x, held, first, total):
    group, rows, width, count = x.shape
    args = (x,) if held is None else (x, held)
    in_specs = [pl.BlockSpec((group, 1, width, count), lambda r: (0, r, 0, 0))]
    if held is not None:
        in_specs.append(pl.BlockSpec(memory_space=pl.ANY))
    return pl.pallas_call(
        unpack_kernel,
        grid=(rows,),
        in_specs=in_specs,
        out_specs=pl.BlockSpec((1, count, group * width), lambda r: (r + first, 0, 0)),
        out_shape=jax.ShapeDtypeStruct((total, count, group * width), x.dtype),
        input_output_aliases={} if held is None else {1: 0},
        cost_estimate=pl.CostEstimate(
            flops=4 * rows * count * group * width, bytes_accessed=4 * rows * count * group * width, transcendentals=0
        ),
    )(*args)


def attend_kernel(heads, low_ref, high_ref, x_ref, dec_ref, enc_ref, o_ref, q_all, k_all, v_all):
    group, _, _, width, count = x_ref.shape
    length = group * count
    row = pl.program_id(0)
    span = min(SPAN, length)
    documents = lax.broadcasted_iota(jnp.int32, (DOCS, length), 0)
    dec_hot = jnp.where(documents == dec_ref[0], 1.0, 0.0).astype(jnp.bfloat16)
    enc_miss = jnp.where(documents == enc_ref[0], 0.0, MASKED).astype(jnp.bfloat16)
    for head in range(heads):
        place = pl.ds(head * HEAD_DIM, HEAD_DIM)
        for part in range(group):
            columns = pl.ds(part * count, count)
            q_all[:HEAD_DIM, columns] = x_ref[part, 0, 0, place]
            v_all[:, columns] = x_ref[part, 2, 0, place]
        q_all[HEAD_DIM:, :] = dec_hot
        for part in range(group):
            columns = slice(part * count, (part + 1) * count)
            both = jnp.concatenate([x_ref[part, 1, 0, place], enc_miss[:, columns]], axis=0)
            k_all[columns, :] = both.T

        def one_span(block):
            at = pl.multiple_of(block * span, span)
            query = q_all[:, pl.ds(at, span)]
            low = low_ref[row, block]
            steps = high_ref[row, block]

            def step(index, held):
                peak, total, summed = held
                start = pl.multiple_of(low + index * span, 128)
                scores = jnp.dot(
                    k_all[pl.ds(start, span), :], query, preferred_element_type=jnp.float32
                )
                fresh = jnp.maximum(peak, jnp.max(scores, axis=0, keepdims=True))
                scale = jnp.exp(peak - fresh)
                expos = jnp.exp(scores - fresh)
                total = total * scale + jnp.sum(expos, axis=0, keepdims=True)
                summed = summed * scale + jnp.dot(
                    v_all[:, pl.ds(start, span)], expos.astype(jnp.bfloat16), preferred_element_type=jnp.float32
                )
                return fresh, total, summed

            init = (
                jnp.full((1, span), 4 * MASKED, jnp.float32),
                jnp.zeros((1, span), jnp.float32),
                jnp.zeros((HEAD_DIM, span), jnp.float32),
            )
            _, total, summed = lax.fori_loop(0, steps, step, init)
            return (summed / total).astype(jnp.bfloat16)

        if count == span:

            def each(block, carry):
                o_ref[block, 0, place] = one_span(block)
                return carry

            lax.fori_loop(0, length // span, each, 0)
        else:
            for block in range(length // span):
                result = one_span(block)
                for piece in range(0, span, count):
                    at = block * span + piece
                    width_here = min(count, span)
                    o_ref[at // count, 0, place, pl.ds(at % count, width_here)] = result[:, piece : piece + width_here]


def tables(dec_rows, enc_rows):
    rows, length = dec_rows.shape
    span = min(SPAN, length)
    docs = dec_rows.reshape(rows, length // span, span)
    before = jnp.sum(enc_rows[:, None, :] < docs[:, :, :1], axis=2, dtype=jnp.int32)
    upto = jnp.sum(enc_rows[:, None, :] <= docs[:, :, -1:], axis=2, dtype=jnp.int32)
    low = before // 128 * 128
    steps = (upto - low + span - 1) // span
    return jnp.minimum(low, length - steps * span), steps


def attend(x, low, steps, dec_rows, enc_rows):
    group, _, rows, width, count = x.shape
    length = group * count
    heads = width // HEAD_DIM
    return pl.pallas_call(
        functools.partial(attend_kernel, heads),
        grid_spec=pltpu.PrefetchScalarGridSpec(
            num_scalar_prefetch=2,
            grid=(rows,),
            in_specs=[
                pl.BlockSpec((group, 3, 1, width, count), lambda r, *_: (0, 0, r, 0, 0)),
                pl.BlockSpec((1, 1, length), lambda r, *_: (r, 0, 0)),
                pl.BlockSpec((1, 1, length), lambda r, *_: (r, 0, 0)),
            ],
            out_specs=pl.BlockSpec((group, 1, width, count), lambda r, *_: (0, r, 0, 0)),
            scratch_shapes=[
                pltpu.VMEM((HEAD_DIM + DOCS, length), jnp.bfloat16),
                pltpu.VMEM((length, HEAD_DIM + DOCS), jnp.bfloat16),
                pltpu.VMEM((HEAD_DIM, length), jnp.bfloat16),
            ],
        ),
        out_shape=jax.ShapeDtypeStruct((group, rows, width, count), x.dtype),
        cost_estimate=pl.CostEstimate(
            flops=rows * heads * length * length * 128,
            bytes_accessed=8 * rows * width * length,
            transcendentals=rows * heads * length * length // 4,
        ),
    )(low, steps, x, dec_rows[:, None, :], enc_rows[:, None, :])


def local(queries, enc_keys, enc_values, dec_ids, enc_ids):
    group = lax.axis_size("seq")
    rows, count, _ = queries.shape
    chunks = CHUNKS if rows % CHUNKS == 0 else 1
    each = rows // chunks
    ids = lax.all_gather(jnp.stack([dec_ids, enc_ids]), "seq", axis=2, tiled=True)
    known = (*tables(ids[0], ids[1]), ids[0], ids[1])

    def exchange(block):
        return lax.all_to_all(block, "seq", split_axis=0, concat_axis=0, tiled=True)

    packed = [pack(queries, enc_keys, enc_values, group, chunk * each, each) for chunk in range(chunks)]
    arrived = [None] * chunks
    attended = [None] * chunks
    arrived[0] = exchange(packed[0])
    if chunks > 1:
        packed[1], known = lax.optimization_barrier((packed[1], known))
        arrived[1] = exchange(packed[1])
    for chunk in range(chunks):
        mine = slice(chunk * each, (chunk + 1) * each)
        attended[chunk] = attend(arrived[chunk], *[table[mine] for table in known])
        if chunk + 2 < chunks:
            packed[chunk + 2], attended[chunk] = lax.optimization_barrier((packed[chunk + 2], attended[chunk]))
            arrived[chunk + 2] = exchange(packed[chunk + 2])
        if chunk + 2 == chunks:
            attended[0], arrived[-1] = lax.optimization_barrier((attended[0], arrived[-1]))
    out = None
    for chunk in range(chunks):
        out = unpack(exchange(attended[chunk]), out, chunk * each, rows)
    return out


def solution(mesh):
    in_specs = (
        P("dp", "seq", None),
        P("dp", "seq", None),
        P("dp", "seq", None),
        P("dp", "seq"),
        P("dp", "seq"),
    )
    out_specs = P("dp", "seq", None)
    return jax.shard_map(local, mesh=mesh, in_specs=in_specs, out_specs=out_specs, check_vma=False)
```

time: 415 us -> 282 us (0.68)
  matrix products: 122 us -> 0 us
  Pallas kernels: 0 us -> 89.9 us
  local copies, waits for them, and re-layouts: 54 us -> 9.04 us
  waiting for transfers between devices: 133 us -> 97.1 us
  other arithmetic: 29 us -> 1.18 us
  starting transfers between devices: 23.1 us -> 32.6 us
    dot_general x64 -> x0, matrix products: 122 us -> none  [the longest x32 75.9 us: attend_dense(): jnp.einsum('qhd,khd->hqk', query_heads[offset:offset + query_span], key_h...]
    pallas_call x0 -> x12, Pallas kernels: none -> 89.9 us  [the longest x4 72.1 us: attend(): pl.pallas_call(functools.partial(attend_kernel, heads), grid_spec=pltpu.P...]
    all_to_all x5 -> x7, waiting for transfers between devices: 133 us -> 97.1 us  [exchange(): return lax.all_to_all(block, 'seq', split_axis=0, concat_axis=0, tiled=True)]
    all_to_all x1, blocking collectives: 51.8 us -> 18.2 us  [exchange(): return lax.all_to_all(block, 'seq', split_axis=0, concat_axis=0, tiled=True)]
    all_gather x0 -> x1, blocking collectives: none -> 32.3 us  [local(): lax.all_gather(jnp.stack([dec_ids, enc_ids]), 'seq', axis=2, tiled=True)]
    reduce_sum x8 -> x1, other arithmetic: 27.4 us -> 0.44 us  [tables(): jnp.sum(enc_rows[:, None, :] < docs[:, :, :1], axis=2, dtype=jnp.int32)]
    unnamed x7 -> x14, local copies, waits for them, and re-layouts: 27.3 us -> 3.35 us
    while x20 -> x0, local copies, waits for them, and re-layouts: 17.8 us -> none  [the longest x4 17.8 us: local(): lax.map(one_row, (query_rows, key_rows, value_rows, dec_rows, enc_rows))]
  transfers between devices with their start and end apart: 5 -> 7, of which waited for: 5 -> 5; matrix products, arithmetic and copies ran while one was open for 6% -> 2% of each run, Pallas kernels for 0% -> 30%
where the time goes in v1:
time: 282 us; the launch traced here: 280 us
  waiting for transfers between devices  97.1 us (34%)
  Pallas kernels  89.9 us (32%)
  blocking collectives  50.5 us (18%)
  starting transfers between devices  32.6 us (12%)
  local copies, waits for them, and re-layouts  9.04 us (3%)
    all_to_all x7, waiting for transfers between devices, exchange(): return lax.all_to_all(block, 'seq', split_axis=0, concat_axis=0, tiled=True)  97.1 us
    pallas_call x4, Pallas kernels, attend(): pl.pallas_call(functools.partial(attend_kernel, heads), grid_spec=pltpu.P...  72.1 us
    all_to_all x7, starting transfers between devices, exchange(): return lax.all_to_all(block, 'seq', split_axis=0, concat_axis=0, tiled=True)  32.6 us
    all_gather x1, blocking collectives, local(): lax.all_gather(jnp.stack([dec_ids, enc_ids]), 'seq', axis=2, tiled=True)  32.3 us
    all_to_all x1, blocking collectives, exchange(): return lax.all_to_all(block, 'seq', split_axis=0, concat_axis=0, tiled=True)  18.2 us
    pallas_call x4, Pallas kernels, pack(): pl.pallas_call(pack_kernel, grid=(rows,), in_specs=[spec] * 3, out_specs=...  10.2 us
    pallas_call x4, Pallas kernels, unpack(): pl.pallas_call(unpack_kernel, grid=(rows,), in_specs=in_specs, out_specs=...  7.66 us
  transfers between devices with their start and end apart: 7, of which 5 were waited for; matrix products, arithmetic and copies ran while one was open for 2% of the time, Pallas kernels for 30%

profile of v1, /device:TPU:0, one launch (start us, length us, event | category | flops | bytes accessed | tf_op | source)
XLA Modules:
  0.0 280.4 jit_solution(6566978151974776654)
XLA Ops:
  0.0 0.7 pad_add_fusion
  0.7 32.3 %all_gather.3 = s32[2,8,2048]{2,1,0:T(8,128)S(1)} all-gather(s32[2,8,256]{2,1,0:T(8,128)S(1)} %pad_add_fusion), channel_id=1, replica_groups=mesh['dp'=4,'seq'=8] {'seq'}, dimensions={2}, use_global_device_ids=true | all-gather | bytes 147456 | tf_op jit(solution)/shard_map/all_gather | solution.py:175
  33.1 0.1 fusion.6
  33.1 0.1 copy.28
  33.3 0.1 copy.27
  33.4 0.4 convert_reduce_fusion.1
  33.9 2.6 shard_map.55
  36.4 5.5 %all-to-all-start.1 = ((bf16[8,3,2,64,256]{4,3,2,1,0:T(8,128)(2,1)}), bf16[8,3,2,64,256]{4,3,2,1,0:T(8,128)(2,1)S(1)}, u32[]{:S(2)}, u32[]{:S(2)}) async-start(bf16[8,3,2,64,256]{4,3,2,1,0:T(8,128)(2,1)} %shard_map.55), calls=%async_computation.1 | async-start | bytes 3145728 | tf_op jit(solution)/shard_map/all_to_all | solution.py:179
  41.9 2.6 shard_map.57
  44.4 28.5 %all-to-all-done.1.x_ref = bf16[8,3,2,64,256]{4,3,2,1,0:T(8,128)(2,1)S(1)} async-done(((bf16[8,3,2,64,256]{4,3,2,1,0:T(8,128)(2,1)}), bf16[8,3,2,64,256]{4,3,2,1,0:T(8,128)(2,1)S(1)}, u32[]{:S(2)}, u32[]{:S(2)}) %all-to-all-start.1) | async-done | bytes 1572896 | tf_op jit(solution)/shard_map/all_to_all | solution.py:179
  72.9 1.1 copy-done.5
  74.1 3.6 %all-to-all-start = ((bf16[8,3,2,64,256]{4,3,2,1,0:T(8,128)(2,1)}), bf16[8,3,2,64,256]{4,3,2,1,0:T(8,128)(2,1)S(1)}, u32[]{:S(2)}, u32[]{:S(2)}) async-start(bf16[8,3,2,64,256]{4,3,2,1,0:T(8,128)(2,1)} %shard_map.57), calls=%async_computation | async-start | bytes 3145728 | tf_op jit(solution)/shard_map/all_to_all | solution.py:179
  77.7 0.6 copy.22.dec_ref
  78.3 0.6 copy.23.enc_ref
  78.9 2.5 shard_map.59
  81.5 0.6 fusion.7
  82.1 19.6 %shard_map.60 = bf16[8,2,64,256]{3,2,1,0:T(8,128)(2,1)} custom-call(s32[2,8]{1,0:T(2,128)} %get-tuple-element.54.low_ref, s32[2,8]{1,0:T(2,128)} %get-tuple-element.45.high_ref, bf16[8,3,2,64,256]{4,3,2,1,0:T(8,128)(2,1)} %copy-done.5, s32[2,1,2048]{2,1,0:T(1,128)} %copy.22.dec_ref, s32[2,1,2048]{2,1,0:T(1,128)} %copy.23.enc_ref), custom_call_target="tpu_custom_call" | custom-call | flops 1073741824 | bytes 2097152 | tf_op jit(solution)/shard_map/pallas_call | solution.py:144
  101.7 11.0 %all-to-all-done.x_ref = bf16[8,3,2,64,256]{4,3,2,1,0:T(8,128)(2,1)S(1)} async-done(((bf16[8,3,2,64,256]{4,3,2,1,0:T(8,128)(2,1)}), bf16[8,3,2,64,256]{4,3,2,1,0:T(8,128)(2,1)S(1)}, u32[]{:S(2)}, u32[]{:S(2)}) %all-to-all-start) | async-done | bytes 1572896 | tf_op jit(solution)/shard_map/all_to_all | solution.py:179
  112.7 18.2 %all_to_all.40.x_ref = bf16[8,2,64,256]{3,2,1,0:T(8,128)(2,1)} all-to-all(bf16[8,2,64,256]{3,2,1,0:T(8,128)(2,1)} %shard_map.60), channel_id=1, replica_groups=mesh['dp'=4,'seq'=8] {'seq'}, dimensions={0} | all-to-all | bytes 1048576 | tf_op jit(solution)/shard_map/all_to_all | solution.py:179
  130.8 3.6 %all-to-all-start.2 = ((bf16[8,3,2,64,256]{4,3,2,1,0:T(8,128)(2,1)}), bf16[8,3,2,64,256]{4,3,2,1,0:T(8,128)(2,1)S(1)}, u32[]{:S(2)}, u32[]{:S(2)}) async-start(bf16[8,3,2,64,256]{4,3,2,1,0:T(8,128)(2,1)} %shard_map.59), calls=%async_computation.2 | async-start | bytes 3145728 | tf_op jit(solution)/shard_map/all_to_all | solution.py:179
  134.5 0.6 copy.20.dec_ref
  135.1 0.6 copy.21.enc_ref
  135.7 2.6 shard_map.56
  138.3 17.6 %shard_map.58 = bf16[8,2,64,256]{3,2,1,0:T(8,128)(2,1)} custom-call(s32[2,8]{1,0:T(2,128)} %get-tuple-element.53.low_ref, s32[2,8]{1,0:T(2,128)} %get-tuple-element.46.high_ref, bf16[8,3,2,64,256]{4,3,2,1,0:T(8,128)(2,1)} %copy-done.4, s32[2,1,2048]{2,1,0:T(1,128)} %copy.20.dec_ref, s32[2,1,2048]{2,1,0:T(1,128)} %copy.21.enc_ref), custom_call_target="tpu_custom_call" | custom-call | flops 1073741824 | bytes 2097152 | tf_op jit(solution)/shard_map/pallas_call | solution.py:144
  155.9 15.2 %all-to-all-done.2.x_ref = bf16[8,3,2,64,256]{4,3,2,1,0:T(8,128)(2,1)S(1)} async-done(((bf16[8,3,2,64,256]{4,3,2,1,0:T(8,128)(2,1)}), bf16[8,3,2,64,256]{4,3,2,1,0:T(8,128)(2,1)S(1)}, u32[]{:S(2)}, u32[]{:S(2)}) %all-to-all-start.2) | async-done | bytes 1572896 | tf_op jit(solution)/shard_map/all_to_all | solution.py:179
  171.1 1.1 copy-done.3
  172.2 4.3 %all-to-all-start.4 = ((bf16[8,3,2,64,256]{4,3,2,1,0:T(8,128)(2,1)}), bf16[8,3,2,64,256]{4,3,2,1,0:T(8,128)(2,1)}, u32[]{:S(2)}, u32[]{:S(2)}) async-start(bf16[8,3,2,64,256]{4,3,2,1,0:T(8,128)(2,1)} %shard_map.56), calls=%async_computation.4 | async-start | bytes 3145728 | tf_op jit(solution)/shard_map/all_to_all | solution.py:179
  176.5 36.7 %all-to-all-done.4.x_ref = bf16[8,3,2,64,256]{4,3,2,1,0:T(8,128)(2,1)} async-done(((bf16[8,3,2,64,256]{4,3,2,1,0:T(8,128)(2,1)}), bf16[8,3,2,64,256]{4,3,2,1,0:T(8,128)(2,1)}, u32[]{:S(2)}, u32[]{:S(2)}) %all-to-all-start.4) | async-done | bytes 1572896 | tf_op jit(solution)/shard_map/all_to_all | solution.py:179
  213.1 3.6 %all-to-all-start.7 = ((bf16[8,2,64,256]{3,2,1,0:T(8,128)(2,1)}), bf16[8,2,64,256]{3,2,1,0:T(8,128)(2,1)S(1)}, u32[]{:S(2)}, u32[]{:S(2)}) async-start(bf16[8,2,64,256]{3,2,1,0:T(8,128)(2,1)} %shard_map.58), calls=%async_computation.7 | async-start | bytes 1048576 | tf_op jit(solution)/shard_map/all_to_all | solution.py:179
  216.8 0.6 copy.26.dec_ref
  217.4 0.6 broadcast_in_dim.31.enc_ref
  218.0 16.8 %shard_map.62 = bf16[8,2,64,256]{3,2,1,0:T(8,128)(2,1)} custom-call(s32[2,8]{1,0:T(2,128)} %get-tuple-element.55.low_ref, s32[2,8]{1,0:T(2,128)} %get-tuple-element.44.high_ref, bf16[8,3,2,64,256]{4,3,2,1,0:T(8,128)(2,1)} %all-to-all-done.4.x_ref, s32[2,1,2048]{2,1,0:T(1,128)} %copy.26.dec_ref, s32[2,1,2048]{2,1,0:T(1,128)} %broadcast_in_dim.31.enc_ref), custom_call_target="tpu_custom_call" | custom-call | flops 1073741824 | bytes 2097152 | tf_op jit(solution)/shard_map/pallas_call | solution.py:144
  234.8 0.0 all-to-all-done.7.x_ref
  234.8 6.0 %all-to-all-start.5 = ((bf16[8,2,64,256]{3,2,1,0:T(8,128)(2,1)}), bf16[8,2,64,256]{3,2,1,0:T(8,128)(2,1)S(1)}, u32[]{:S(2)}, u32[]{:S(2)}) async-start(bf16[8,2,64,256]{3,2,1,0:T(8,128)(2,1)} %shard_map.62), calls=%async_computation.5 | async-start | bytes 1048576 | tf_op jit(solution)/shard_map/all_to_all | solution.py:179
  240.8 0.6 copy.24.dec_ref
  241.4 0.6 copy.25.enc_ref
  242.0 18.0 %shard_map.61 = bf16[8,2,64,256]{3,2,1,0:T(8,128)(2,1)} custom-call(s32[2,8]{1,0:T(2,128)} %get-tuple-element.52.low_ref, s32[2,8]{1,0:T(2,128)} %get-tuple-element.47.high_ref, bf16[8,3,2,64,256]{4,3,2,1,0:T(8,128)(2,1)} %copy-done.3, s32[2,1,2048]{2,1,0:T(1,128)} %copy.24.dec_ref, s32[2,1,2048]{2,1,0:T(1,128)} %copy.25.enc_ref), custom_call_target="tpu_custom_call" | custom-call | flops 1073741824 | bytes 2097152 | tf_op jit(solution)/shard_map/pallas_call | solution.py:144
  260.1 0.0 copy-done
  260.1 0.0 all-to-all-done.5.x_ref
  260.1 0.0 copy-start.1
  260.1 6.0 %all-to-all-start.3 = ((bf16[8,2,64,256]{3,2,1,0:T(8,128)(2,1)}), bf16[8,2,64,256]{3,2,1,0:T(8,128)(2,1)S(1)}, u32[]{:S(2)}, u32[]{:S(2)}) async-start(bf16[8,2,64,256]{3,2,1,0:T(8,128)(2,1)} %shard_map.61), calls=%async_computation.3 | async-start | bytes 1048576 | tf_op jit(solution)/shard_map/all_to_all | solution.py:179
  266.1 1.9 shard_map.63.rest_0_
  268.0 0.0 copy-done.1
  268.0 1.9 shard_map.64.rest_0_
  269.9 1.9 shard_map.65.rest_0_
  271.9 5.8 %all-to-all-done.3.x_ref = bf16[8,2,64,256]{3,2,1,0:T(8,128)(2,1)S(1)} async-done(((bf16[8,2,64,256]{3,2,1,0:T(8,128)(2,1)}), bf16[8,2,64,256]{3,2,1,0:T(8,128)(2,1)S(1)}, u32[]{:S(2)}, u32[]{:S(2)}) %all-to-all-start.3) | async-done | bytes 524320 | tf_op jit(solution)/shard_map/all_to_all | solution.py:179
  277.7 0.8 copy-done.2
  278.5 1.9 shard_map.66
  (10 shorter events, 0.1 us)
Async XLA Ops:
  36.4 36.5 %all-to-all-start.1 = ((bf16[8,3,2,64,256]{4,3,2,1,0:T(8,128)(2,1)}), bf16[8,3,2,64,256]{4,3,2,1,0:T(8,128)(2,1)S(1)}, u32[]{:S(2)}, u32[]{:S(2)}) async-start(bf16[8,3,2,64,256]{4,3,2,1,0:T(8,128)(2,1)} %shard_map.55), calls=%async_computation.1 | async-start | bytes 3145728 | tf_op jit(solution)/shard_map/all_to_all | solution.py:179
  72.9 1.1 copy-start.5
  74.1 38.6 %all-to-all-start = ((bf16[8,3,2,64,256]{4,3,2,1,0:T(8,128)(2,1)}), bf16[8,3,2,64,256]{4,3,2,1,0:T(8,128)(2,1)S(1)}, u32[]{:S(2)}, u32[]{:S(2)}) async-start(bf16[8,3,2,64,256]{4,3,2,1,0:T(8,128)(2,1)} %shard_map.57), calls=%async_computation | async-start | bytes 3145728 | tf_op jit(solution)/shard_map/all_to_all | solution.py:179
  112.7 18.2 %copy-start.4 = (bf16[8,3,2,64,256]{4,3,2,1,0:T(8,128)(2,1)}, bf16[8,3,2,64,256]{4,3,2,1,0:T(8,128)(2,1)S(1)}, u32[]{:S(2)}) copy-start(bf16[8,3,2,64,256]{4,3,2,1,0:T(8,128)(2,1)S(1)} %all-to-all-done.x_ref) | copy-start | bytes 4718596
  130.8 40.2 %all-to-all-start.2 = ((bf16[8,3,2,64,256]{4,3,2,1,0:T(8,128)(2,1)}), bf16[8,3,2,64,256]{4,3,2,1,0:T(8,128)(2,1)S(1)}, u32[]{:S(2)}, u32[]{:S(2)}) async-start(bf16[8,3,2,64,256]{4,3,2,1,0:T(8,128)(2,1)} %shard_map.59), calls=%async_computation.2 | async-start | bytes 3145728 | tf_op jit(solution)/shard_map/all_to_all | solution.py:179
  171.1 1.1 copy-start.3
  172.2 40.9 %all-to-all-start.4 = ((bf16[8,3,2,64,256]{4,3,2,1,0:T(8,128)(2,1)}), bf16[8,3,2,64,256]{4,3,2,1,0:T(8,128)(2,1)}, u32[]{:S(2)}, u32[]{:S(2)}) async-start(bf16[8,3,2,64,256]{4,3,2,1,0:T(8,128)(2,1)} %shard_map.56), calls=%async_computation.4 | async-start | bytes 3145728 | tf_op jit(solution)/shard_map/all_to_all | solution.py:179
  213.1 21.7 %all-to-all-start.7 = ((bf16[8,2,64,256]{3,2,1,0:T(8,128)(2,1)}), bf16[8,2,64,256]{3,2,1,0:T(8,128)(2,1)S(1)}, u32[]{:S(2)}, u32[]{:S(2)}) async-start(bf16[8,2,64,256]{3,2,1,0:T(8,128)(2,1)} %shard_map.58), calls=%async_computation.7 | async-start | bytes 1048576 | tf_op jit(solution)/shard_map/all_to_all | solution.py:179
  234.8 25.3 %copy-start = (bf16[8,2,64,256]{3,2,1,0:T(8,128)(2,1)}, bf16[8,2,64,256]{3,2,1,0:T(8,128)(2,1)S(1)}, u32[]{:S(2)}) copy-start(bf16[8,2,64,256]{3,2,1,0:T(8,128)(2,1)S(1)} %all-to-all-done.7.x_ref) | copy-start | bytes 1572868
  234.8 25.3 %all-to-all-start.5 = ((bf16[8,2,64,256]{3,2,1,0:T(8,128)(2,1)}), bf16[8,2,64,256]{3,2,1,0:T(8,128)(2,1)S(1)}, u32[]{:S(2)}, u32[]{:S(2)}) async-start(bf16[8,2,64,256]{3,2,1,0:T(8,128)(2,1)} %shard_map.62), calls=%async_computation.5 | async-start | bytes 1048576 | tf_op jit(solution)/shard_map/all_to_all | solution.py:179
  260.1 7.9 %copy-start.1 = (bf16[8,2,64,256]{3,2,1,0:T(8,128)(2,1)}, bf16[8,2,64,256]{3,2,1,0:T(8,128)(2,1)S(1)}, u32[]{:S(2)}) copy-start(bf16[8,2,64,256]{3,2,1,0:T(8,128)(2,1)S(1)} %all-to-all-done.5.x_ref) | copy-start | bytes 1572868
  260.1 17.6 %all-to-all-start.3 = ((bf16[8,2,64,256]{3,2,1,0:T(8,128)(2,1)}), bf16[8,2,64,256]{3,2,1,0:T(8,128)(2,1)S(1)}, u32[]{:S(2)}, u32[]{:S(2)}) async-start(bf16[8,2,64,256]{3,2,1,0:T(8,128)(2,1)} %shard_map.61), calls=%async_computation.3 | async-start | bytes 1048576 | tf_op jit(solution)/shard_map/all_to_all | solution.py:179
  277.7 0.8 copy-start.2

commit v2 on v1

--- a/solution.py
+++ b/solution.py
@@ -9,31 +9,40 @@
 
 HEAD_DIM = 64
 DOCS = 16
-CHUNKS = 4
 SPAN = 256
 MASKED = -8192.0
 
 
-def pack_kernel(q_ref, k_ref, v_ref, o_ref):
-    group, _, _, width, count = o_ref.shape
-    for slot, ref in enumerate((q_ref, k_ref, v_ref)):
-        o_ref[:, slot, 0] = ref[0].T.reshape(group, width, count)
-
-
-def pack(q, k, v, group, first, rows):
+def pack_kernel(rows, q_ref, k_ref, v_ref, ids_ref, o_ref):
+    group, _, count = o_ref.shape
+    width = q_ref.shape[2] // group
+
+    @pl.when(pl.program_id(0) < rows)
+    def _():
+        for slot, ref in enumerate((q_ref, k_ref, v_ref)):
+            o_ref[:, slot * width : (slot + 1) * width] = ref[0].T.reshape(group, width, count)
+
+    @pl.when(pl.program_id(0) == rows)
+    def _():
+        for target in range(group):
+            o_ref[target, : ids_ref.shape[0]] = ids_ref[...]
+
+
+def pack(q, k, v, ids, group, first, rows, with_ids):
     _, count, features = q.shape
     width = features // group
-    spec = pl.BlockSpec((1, count, features), lambda r: (r + first, 0, 0))
+    spec = pl.BlockSpec((1, count, features), lambda r: (jnp.minimum(r, rows - 1) + first, 0, 0))
+    more = ids.shape[0] if with_ids else 0
     return pl.pallas_call(
-        pack_kernel,
-        grid=(rows,),
-        in_specs=[spec] * 3,
-        out_specs=pl.BlockSpec((group, 3, 1, width, count), lambda r: (0, 0, r, 0, 0)),
-        out_shape=jax.ShapeDtypeStruct((group, 3, rows, width, count), q.dtype),
+        functools.partial(pack_kernel, rows),
+        grid=(rows + 1 if with_ids else rows,),
+        in_specs=[spec] * 3 + [pl.BlockSpec(ids.shape, lambda r: (0, 0))],
+        out_specs=pl.BlockSpec((group, 3 * width, count), lambda r: (0, r, 0)),
+        out_shape=jax.ShapeDtypeStruct((group, rows * 3 * width + more, count), q.dtype),
         cost_estimate=pl.CostEstimate(
             flops=4 * rows * count * features, bytes_accessed=12 * rows * count * features, transcendentals=0
         ),
-    )(q, k, v)
+    )(q, k, v, ids)
 
 
 def unpack_kernel(x_ref, *rest):
@@ -62,7 +71,8 @@
 
 
 def attend_kernel(heads, low_ref, high_ref, x_ref, dec_ref, enc_ref, o_ref, q_all, k_all, v_all):
-    group, _, _, width, count = x_ref.shape
+    group, stacked, count = x_ref.shape
+    width = stacked // 3
     length = group * count
     row = pl.program_id(0)
     span = min(SPAN, length)
@@ -73,12 +83,12 @@
         place = pl.ds(head * HEAD_DIM, HEAD_DIM)
         for part in range(group):
             columns = pl.ds(part * count, count)
-            q_all[:HEAD_DIM, columns] = x_ref[part, 0, 0, place]
-            v_all[:, columns] = x_ref[part, 2, 0, place]
+            q_all[:HEAD_DIM, columns] = x_ref[part, place]
+            v_all[:, columns] = x_ref[part, pl.ds(2 * width + head * HEAD_DIM, HEAD_DIM)]
         q_all[HEAD_DIM:, :] = dec_hot
         for part in range(group):
             columns = slice(part * count, (part + 1) * count)
-            both = jnp.concatenate([x_ref[part, 1, 0, place], enc_miss[:, columns]], axis=0)
+            both = jnp.concatenate([x_ref[part, pl.ds(width + head * HEAD_DIM, HEAD_DIM)], enc_miss[:, columns]], axis=0)
             k_all[columns, :] = both.T
 
         def one_span(block):
@@ -137,8 +147,9 @@
     return jnp.minimum(low, length - steps * span), steps
 
 
-def attend(x, low, steps, dec_rows, enc_rows):
-    group, _, rows, width, count = x.shape
+def attend(x, width, low, steps, dec_rows, enc_rows):
+    group, _, count = x.shape
+    rows = low.shape[0]
     length = group * count
     heads = width // HEAD_DIM
     return pl.pallas_call(
@@ -147,7 +158,7 @@
             num_scalar_prefetch=2,
             grid=(rows,),
             in_specs=[
-                pl.BlockSpec((group, 3, 1, width, count), lambda r, *_: (0, 0, r, 0, 0)),
+                pl.BlockSpec((group, 3 * width, count), lambda r, *_: (0, r, 0)),
                 pl.BlockSpec((1, 1, length), lambda r, *_: (r, 0, 0)),
                 pl.BlockSpec((1, 1, length), lambda r, *_: (r, 0, 0)),
             ],
@@ -169,33 +180,26 @@
 
 def local(queries, enc_keys, enc_values, dec_ids, enc_ids):
     group = lax.axis_size("seq")
-    rows, count, _ = queries.shape
-    chunks = CHUNKS if rows % CHUNKS == 0 else 1
-    each = rows // chunks
-    ids = lax.all_gather(jnp.stack([dec_ids, enc_ids]), "seq", axis=2, tiled=True)
-    known = (*tables(ids[0], ids[1]), ids[0], ids[1])
+    rows, count, features = queries.shape
+    width = features // group
+    early = max(1, rows * 5 // 8)
+    cuts = [(0, early), (early, rows - early)] if rows > 1 else [(0, rows)]
+    ids = jnp.concatenate([dec_ids, enc_ids], axis=0).astype(queries.dtype)
 
     def exchange(block):
         return lax.all_to_all(block, "seq", split_axis=0, concat_axis=0, tiled=True)
 
-    packed = [pack(queries, enc_keys, enc_values, group, chunk * each, each) for chunk in range(chunks)]
-    arrived = [None] * chunks
-    attended = [None] * chunks
-    arrived[0] = exchange(packed[0])
-    if chunks > 1:
-        packed[1], known = lax.optimization_barrier((packed[1], known))
-        arrived[1] = exchange(packed[1])
-    for chunk in range(chunks):
-        mine = slice(chunk * each, (chunk + 1) * each)
-        attended[chunk] = attend(arrived[chunk], *[table[mine] for table in known])
-        if chunk + 2 < chunks:
-            packed[chunk + 2], attended[chunk] = lax.optimization_barrier((packed[chunk + 2], attended[chunk]))
-            arrived[chunk + 2] = exchange(packed[chunk + 2])
-        if chunk + 2 == chunks:
-            attended[0], arrived[-1] = lax.optimization_barrier((attended[0], arrived[-1]))
+    arrived = [
+        exchange(pack(queries, enc_keys, enc_values, ids, group, first, size, first == 0)) for first, size in cuts
+    ]
+    spread = arrived[0][:, early * 3 * width :].astype(jnp.int32)
+    whole_rows = spread.transpose(1, 0, 2).reshape(2 * rows, group * count)
+    dec_rows, enc_rows = whole_rows[:rows], whole_rows[rows:]
+    known = (*tables(dec_rows, enc_rows), dec_rows, enc_rows)
     out = None
-    for chunk in range(chunks):
-        out = unpack(exchange(attended[chunk]), out, chunk * each, rows)
+    for (first, size), block in zip(cuts, arrived):
+        attended = attend(block, width, *[table[first : first + size] for table in known])
+        out = unpack(exchange(attended), out, first, rows)
     return out
 
 

time: 282 us -> 228 us (0.81)
  blocking collectives: 50.5 us -> 0 us
  waiting for transfers between devices: 97.1 us -> 120 us
  starting transfers between devices: 32.6 us -> 18.2 us
  Pallas kernels: 89.9 us -> 78.2 us
    all_gather x1 -> x0, blocking collectives: 32.3 us -> none  [local(): lax.all_gather(jnp.stack([dec_ids, enc_ids]), 'seq', axis=2, tiled=True)]
    all_to_all x7 -> x4, waiting for transfers between devices: 97.1 us -> 120 us  [exchange(): return lax.all_to_all(block, 'seq', split_axis=0, concat_axis=0, tiled=True)]
    all_to_all x1 -> x0, blocking collectives: 18.2 us -> none  [exchange(): return lax.all_to_all(block, 'seq', split_axis=0, concat_axis=0, tiled=True)]
    all_to_all x7 -> x4, starting transfers between devices: 32.6 us -> 18.2 us  [exchange(): return lax.all_to_all(block, 'seq', split_axis=0, concat_axis=0, tiled=True)]
    pallas_call x4 -> x2, Pallas kernels: 72.1 us -> 60.4 us  [attend(): pl.pallas_call(functools.partial(attend_kernel, heads), grid_spec=pltpu.P...]
    pallas_call x4 -> x2, Pallas kernels: 7.66 us -> 7.27 us  [unpack(): pl.pallas_call(unpack_kernel, grid=(rows,), in_specs=in_specs, out_specs=...]
    pallas_call x4 -> x2, Pallas kernels: 10.2 us -> 10.5 us  [pack(): pl.pallas_call(functools.partial(pack_kernel, rows), grid=(rows + 1 if wi...]
  transfers between devices with their start and end apart: 7 -> 4, of which waited for: 5 -> 4; matrix products, arithmetic and copies ran while one was open for 2% -> 3% of each run, Pallas kernels for 30% -> 30%
where the time goes in v2:
time: 228 us; the launch traced here: 227 us
  waiting for transfers between devices  120 us (53%)
  Pallas kernels  78.2 us (34%)
  starting transfers between devices  18.2 us (8%)
  local copies, waits for them, and re-layouts  6.49 us (3%)
  other arithmetic  3.91 us (2%)
    all_to_all x4, waiting for transfers between devices, exchange(): return lax.all_to_all(block, 'seq', split_axis=0, concat_axis=0, tiled=True)  120 us
    pallas_call x2, Pallas kernels, attend(): pl.pallas_call(functools.partial(attend_kernel, heads), grid_spec=pltpu.P...  60.4 us
    all_to_all x4, starting transfers between devices, exchange(): return lax.all_to_all(block, 'seq', split_axis=0, concat_axis=0, tiled=True)  18.2 us
    pallas_call x2, Pallas kernels, pack(): pl.pallas_call(functools.partial(pack_kernel, rows), grid=(rows + 1 if wi...  10.5 us
    pallas_call x2, Pallas kernels, unpack(): pl.pallas_call(unpack_kernel, grid=(rows,), in_specs=in_specs, out_specs=...  7.27 us
  transfers between devices with their start and end apart: 4, of which 4 were waited for; matrix products, arithmetic and copies ran while one was open for 3% of the time, Pallas kernels for 30%

profile of v2, /device:TPU:0, one launch (start us, length us, event | category | flops | bytes accessed | tf_op | source)
XLA Modules:
  0.0 226.8 jit_solution(11889193197055497900)
XLA Ops:
  0.0 0.7 convert.7
  0.7 0.7 convert.8
  1.4 0.6 pad_maximum_fusion.ids_ref
  2.0 6.2 %shard_map.55 = bf16[8,976,256]{2,1,0:T(8,128)(2,1)} custom-call(bf16[8,256,512]{2,1,0:T(8,128)(2,1)} %q_ref.3, bf16[8,256,512]{2,1,0:T(8,128)(2,1)} %k_ref.3, bf16[8,256,512]{2,1,0:T(8,128)(2,1)} %v_ref.3, bf16[16,256]{1,0:T(8,128)(2,1)} %pad_maximum_fusion.ids_ref), custom_call_target="tpu_custom_call" | custom-call | flops 2621440 | bytes 7864320 | tf_op jit(solution)/shard_map/pallas_call | solution.py:36
  8.3 7.3 %all-to-all-start = ((bf16[8,976,256]{2,1,0:T(8,128)(2,1)}), bf16[8,976,256]{2,1,0:T(8,128)(2,1)}, u32[]{:S(2)}, u32[]{:S(2)}) async-start(bf16[8,976,256]{2,1,0:T(8,128)(2,1)} %shard_map.55), calls=%async_computation | async-start | bytes 7995392 | tf_op jit(solution)/shard_map/all_to_all | solution.py:190
  15.5 4.2 %shard_map.56 = bf16[8,576,256]{2,1,0:T(8,128)(2,1)} custom-call(bf16[8,256,512]{2,1,0:T(8,128)(2,1)} %q_ref.3, bf16[8,256,512]{2,1,0:T(8,128)(2,1)} %k_ref.3, bf16[8,256,512]{2,1,0:T(8,128)(2,1)} %v_ref.3, bf16[16,256]{1,0:T(8,128)(2,1)} %pad_maximum_fusion.ids_ref), custom_call_target="tpu_custom_call" | custom-call | flops 1572864 | bytes 4718592 | tf_op jit(solution)/shard_map/pallas_call | solution.py:36
  19.8 84.8 %all-to-all-done.x_ref = bf16[8,976,256]{2,1,0:T(8,128)(2,1)} async-done(((bf16[8,976,256]{2,1,0:T(8,128)(2,1)}), bf16[8,976,256]{2,1,0:T(8,128)(2,1)}, u32[]{:S(2)}, u32[]{:S(2)}) %all-to-all-start) | async-done | bytes 3997728 | tf_op jit(solution)/shard_map/all_to_all | solution.py:190
  104.6 3.6 %all-to-all-start.1 = ((bf16[8,576,256]{2,1,0:T(8,128)(2,1)}), bf16[8,576,256]{2,1,0:T(8,128)(2,1)S(1)}, u32[]{:S(2)}, u32[]{:S(2)}) async-start(bf16[8,576,256]{2,1,0:T(8,128)(2,1)} %shard_map.56), calls=%async_computation.1 | async-start | bytes 4718592 | tf_op jit(solution)/shard_map/all_to_all | solution.py:190
  108.2 0.9 convert_bitcast_fusion
  109.1 0.1 fusion.7
  109.2 0.1 copy.17
  109.3 0.1 copy.18
  109.5 0.7 broadcast_in_dim.16.dec_ref
  110.2 0.7 broadcast_in_dim.17.enc_ref
  110.8 0.4 convert_reduce_fusion.1
  111.3 0.6 subtract_minimum_fusion
  111.9 38.0 %shard_map.58 = bf16[8,5,64,256]{3,2,1,0:T(8,128)(2,1)} custom-call(s32[5,8]{1,0:T(8,128)} %bitcast.15, s32[5,8]{1,0:T(8,128)} %bitcast.14, bf16[8,976,256]{2,1,0:T(8,128)(2,1)} %all-to-all-done.x_ref, s32[5,1,2048]{2,1,0:T(1,128)} %broadcast_in_dim.16.dec_ref, s32[5,1,2048]{2,1,0:T(1,128)} %broadcast_in_dim.17.enc_ref), custom_call_target="tpu_custom_call" | custom-call | flops 2684354560 | bytes 5242880 | tf_op jit(solution)/shard_map/pallas_call | solution.py:155
  149.9 0.0 copy-start.4
  149.9 0.0 copy-start.3
  149.9 12.4 %all-to-all-done.1.x_ref = bf16[8,576,256]{2,1,0:T(8,128)(2,1)S(1)} async-done(((bf16[8,576,256]{2,1,0:T(8,128)(2,1)}), bf16[8,576,256]{2,1,0:T(8,128)(2,1)S(1)}, u32[]{:S(2)}, u32[]{:S(2)}) %all-to-all-start.1) | async-done | bytes 2359328 | tf_op jit(solution)/shard_map/all_to_all | solution.py:190
  162.3 0.0 copy-start.2
  162.3 1.4 copy-done.2
  163.7 3.6 %all-to-all-start.3 = ((bf16[8,5,64,256]{3,2,1,0:T(8,128)(2,1)}), bf16[8,5,64,256]{3,2,1,0:T(8,128)(2,1)S(1)}, u32[]{:S(2)}, u32[]{:S(2)}) async-start(bf16[8,5,64,256]{3,2,1,0:T(8,128)(2,1)} %shard_map.58), calls=%async_computation.3 | async-start | bytes 2621440 | tf_op jit(solution)/shard_map/all_to_all | solution.py:190
  167.3 0.0 copy-done.4
  167.3 0.6 slice.53.low_ref
  167.9 0.0 copy-done.3
  167.9 0.6 slice.54.high_ref
  168.6 0.6 copy.19.dec_ref
  169.2 0.6 copy.20.enc_ref
  169.8 22.4 %shard_map.57 = bf16[8,3,64,256]{3,2,1,0:T(8,128)(2,1)} custom-call(s32[3,8]{1,0:T(4,128)} %slice.53.low_ref, s32[3,8]{1,0:T(4,128)} %slice.54.high_ref, bf16[8,576,256]{2,1,0:T(8,128)(2,1)} %copy-done.2, s32[3,1,2048]{2,1,0:T(1,128)} %copy.19.dec_ref, s32[3,1,2048]{2,1,0:T(1,128)} %copy.20.enc_ref), custom_call_target="tpu_custom_call" | custom-call | flops 1610612736 | bytes 3145728 | tf_op jit(solution)/shard_map/pallas_call | solution.py:155
  192.3 6.7 %all-to-all-done.3.x_ref = bf16[8,5,64,256]{3,2,1,0:T(8,128)(2,1)S(1)} async-done(((bf16[8,5,64,256]{3,2,1,0:T(8,128)(2,1)}), bf16[8,5,64,256]{3,2,1,0:T(8,128)(2,1)S(1)}, u32[]{:S(2)}, u32[]{:S(2)}) %all-to-all-start.3) | async-done | bytes 1310752 | tf_op jit(solution)/shard_map/all_to_all | solution.py:190
  198.9 0.0 copy-start
  198.9 3.6 %all-to-all-start.2 = ((bf16[8,3,64,256]{3,2,1,0:T(8,128)(2,1)}), bf16[8,3,64,256]{3,2,1,0:T(8,128)(2,1)S(1)}, u32[]{:S(2)}, u32[]{:S(2)}) async-start(bf16[8,3,64,256]{3,2,1,0:T(8,128)(2,1)} %shard_map.57), calls=%async_computation.2 | async-start | bytes 1572864 | tf_op jit(solution)/shard_map/all_to_all | solution.py:190
  202.5 0.0 copy-done
  202.6 4.2 %shard_map.59.rest_0_ = bf16[8,256,512]{2,1,0:T(8,128)(2,1)} custom-call(bf16[8,5,64,256]{3,2,1,0:T(8,128)(2,1)} %copy-done), custom_call_target="tpu_custom_call" | custom-call | flops 2621440 | bytes 2621440 | tf_op jit(solution)/shard_map/pallas_call | solution.py:60
  206.8 16.1 %all-to-all-done.2.x_ref = bf16[8,3,64,256]{3,2,1,0:T(8,128)(2,1)S(1)} async-done(((bf16[8,3,64,256]{3,2,1,0:T(8,128)(2,1)}), bf16[8,3,64,256]{3,2,1,0:T(8,128)(2,1)S(1)}, u32[]{:S(2)}, u32[]{:S(2)}) %all-to-all-start.2) | async-done | bytes 786464 | tf_op jit(solution)/shard_map/all_to_all | solution.py:190
  222.9 0.0 copy-start.1
  222.9 0.9 copy-done.1
  223.8 3.0 %shard_map.60 = bf16[8,256,512]{2,1,0:T(8,128)(2,1)} custom-call(bf16[8,3,64,256]{3,2,1,0:T(8,128)(2,1)} %copy-done.1, bf16[8,256,512]{2,1,0:T(8,128)(2,1)} %shard_map.59.rest_0_), custom_call_target="tpu_custom_call", output_to_operand_aliasing={{}: (1, {})} | custom-call | flops 1572864 | bytes 1572864 | tf_op jit(solution)/shard_map/pallas_call | solution.py:60
  (5 shorter events, 0.1 us)
Async XLA Ops:
  8.3 96.4 %all-to-all-start = ((bf16[8,976,256]{2,1,0:T(8,128)(2,1)}), bf16[8,976,256]{2,1,0:T(8,128)(2,1)}, u32[]{:S(2)}, u32[]{:S(2)}) async-start(bf16[8,976,256]{2,1,0:T(8,128)(2,1)} %shard_map.55), calls=%async_computation | async-start | bytes 7995392 | tf_op jit(solution)/shard_map/all_to_all | solution.py:190
  104.6 57.7 %all-to-all-start.1 = ((bf16[8,576,256]{2,1,0:T(8,128)(2,1)}), bf16[8,576,256]{2,1,0:T(8,128)(2,1)S(1)}, u32[]{:S(2)}, u32[]{:S(2)}) async-start(bf16[8,576,256]{2,1,0:T(8,128)(2,1)} %shard_map.56), calls=%async_computation.1 | async-start | bytes 4718592 | tf_op jit(solution)/shard_map/all_to_all | solution.py:190
  149.9 17.4 %copy-start.4 = (s32[8,8]{1,0:T(8,128)S(1)}, s32[8,8]{1,0:T(8,128)}, u32[]{:S(2)}) copy-start(s32[8,8]{1,0:T(8,128)} %get-tuple-element.7) | copy-start | bytes 772
  149.9 18.0 %copy-start.3 = (s32[8,8]{1,0:T(8,128)S(1)}, s32[8,8]{1,0:T(8,128)}, u32[]{:S(2)}) copy-start(s32[8,8]{1,0:T(8,128)} %get-tuple-element.8) | copy-start | bytes 772
  162.3 1.4 copy-start.2
  163.7 35.2 %all-to-all-start.3 = ((bf16[8,5,64,256]{3,2,1,0:T(8,128)(2,1)}), bf16[8,5,64,256]{3,2,1,0:T(8,128)(2,1)S(1)}, u32[]{:S(2)}, u32[]{:S(2)}) async-start(bf16[8,5,64,256]{3,2,1,0:T(8,128)(2,1)} %shard_map.58), calls=%async_computation.3 | async-start | bytes 2621440 | tf_op jit(solution)/shard_map/all_to_all | solution.py:190
  198.9 3.6 %copy-start = (bf16[8,5,64,256]{3,2,1,0:T(8,128)(2,1)}, bf16[8,5,64,256]{3,2,1,0:T(8,128)(2,1)S(1)}, u32[]{:S(2)}) copy-start(bf16[8,5,64,256]{3,2,1,0:T(8,128)(2,1)S(1)} %all-to-all-done.3.x_ref) | copy-start | bytes 3932164
  198.9 24.0 %all-to-all-start.2 = ((bf16[8,3,64,256]{3,2,1,0:T(8,128)(2,1)}), bf16[8,3,64,256]{3,2,1,0:T(8,128)(2,1)S(1)}, u32[]{:S(2)}, u32[]{:S(2)}) async-start(bf16[8,3,64,256]{3,2,1,0:T(8,128)(2,1)} %shard_map.57), calls=%async_computation.2 | async-start | bytes 1572864 | tf_op jit(solution)/shard_map/all_to_all | solution.py:190
  222.9 0.9 copy-start.1

commit v3 on v2

--- a/solution.py
+++ b/solution.py
@@ -43,6 +43,75 @@
             flops=4 * rows * count * features, bytes_accessed=12 * rows * count * features, transcendentals=0
         ),
     )(q, k, v, ids)
+
+
+def deliver_kernel(group, x_ref, q_ref, k_ref, v_ref, o_ref, p_ref, held, own_sem, send_sem, recv_sem):
+    me = lax.axis_index("seq")
+
+    def transfer(shift):
+        target = lax.rem(me + shift, group)
+        return pltpu.make_async_remote_copy(
+            src_ref=x_ref.at[target],
+            dst_ref=o_ref.at[me],
+            send_sem=send_sem.at[shift - 1],
+            recv_sem=recv_sem.at[shift - 1],
+            device_id={"seq": target},
+            device_id_type=pl.DeviceIdType.MESH,
+        )
+
+    @pl.when(pl.program_id(0) == 0)
+    def _():
+        barrier = pltpu.get_barrier_semaphore()
+        for shift in range(1, group):
+            pl.semaphore_signal(
+                barrier, inc=1, device_id={"seq": lax.rem(me + shift, group)}, device_id_type=pl.DeviceIdType.MESH
+            )
+        pl.semaphore_wait(barrier, group - 1)
+        for shift in range(1, group):
+            transfer(shift).start()
+        own = pltpu.make_async_copy(x_ref.at[me], held, own_sem)
+        own.start()
+        own.wait()
+        own = pltpu.make_async_copy(held, o_ref.at[me], own_sem)
+        own.start()
+        own.wait()
+
+    _, _, count = p_ref.shape
+    width = q_ref.shape[2] // group
+    for slot, ref in enumerate((q_ref, k_ref, v_ref)):
+        p_ref[:, slot * width : (slot + 1) * width] = ref[0].T.reshape(group, width, count)
+
+    @pl.when(pl.program_id(0) == pl.num_programs(0) - 1)
+    def _():
+        for shift in range(1, group):
+            transfer(shift).wait()
+
+
+def deliver(x, q, k, v, first, rows):
+    group = x.shape[0]
+    _, count, features = q.shape
+    width = features // group
+    spec = pl.BlockSpec((1, count, features), lambda r: (r + first, 0, 0))
+    return pl.pallas_call(
+        functools.partial(deliver_kernel, group),
+        grid=(rows,),
+        in_specs=[pl.BlockSpec(memory_space=pl.ANY)] + [spec] * 3,
+        out_specs=(
+            pl.BlockSpec(memory_space=pl.ANY),
+            pl.BlockSpec((group, 3 * width, count), lambda r: (0, r, 0)),
+        ),
+        out_shape=(
+            jax.ShapeDtypeStruct(x.shape, x.dtype),
+            jax.ShapeDtypeStruct((group, rows * 3 * width, count), x.dtype),
+        ),
+        scratch_shapes=[
+            pltpu.VMEM(x.shape[1:], x.dtype),
+            pltpu.SemaphoreType.DMA,
+            pltpu.SemaphoreType.DMA((group - 1,)),
+            pltpu.SemaphoreType.DMA((group - 1,)),
+        ],
+        compiler_params=pltpu.CompilerParams(collective_id=0, has_side_effects=True),
+    )(x, q, k, v)
 
 
 def unpack_kernel(x_ref, *rest):
@@ -189,9 +258,13 @@
     def exchange(block):
         return lax.all_to_all(block, "seq", split_axis=0, concat_axis=0, tiled=True)
 
-    arrived = [
-        exchange(pack(queries, enc_keys, enc_values, ids, group, first, size, first == 0)) for first, size in cuts
-    ]
+    packed = pack(queries, enc_keys, enc_values, ids, group, *cuts[0], True)
+    if group > 1 and rows > 1:
+        whole, packed = deliver(packed, queries, enc_keys, enc_values, *cuts[1])
+        arrived = [whole, exchange(packed)]
+    else:
+        arrived = [exchange(packed)]
+        arrived += [exchange(pack(queries, enc_keys, enc_values, ids, group, *cut, False)) for cut in cuts[1:]]
     spread = arrived[0][:, early * 3 * width :].astype(jnp.int32)
     whole_rows = spread.transpose(1, 0, 2).reshape(2 * rows, group * count)
     dec_rows, enc_rows = whole_rows[:rows], whole_rows[rows:]

time: 228 us -> 226 us (level)
  waiting for transfers between devices: 120 us -> 31.8 us
  Pallas kernels: 78.2 us -> 149 us
  starting transfers between devices: 18.2 us -> 34.2 us
    all_to_all x4 -> x3, waiting for transfers between devices: 120 us -> 31.8 us  [exchange(): return lax.all_to_all(block, 'seq', split_axis=0, concat_axis=0, tiled=True)]
    pallas_call x0 -> x1, Pallas kernels: none -> 72.7 us  [deliver(): pl.pallas_call(functools.partial(deliver_kernel, group), grid=(rows,), in...]
    all_to_all x4 -> x3, starting transfers between devices: 18.2 us -> 34.2 us  [exchange(): return lax.all_to_all(block, 'seq', split_axis=0, concat_axis=0, tiled=True)]
    pallas_call x2 -> x1, Pallas kernels: 10.5 us -> 6.22 us  [pack(): pl.pallas_call(functools.partial(pack_kernel, rows), grid=(rows + 1 if wi...]
    pallas_call x2, Pallas kernels: 60.4 us -> 62.8 us  [attend(): pl.pallas_call(functools.partial(attend_kernel, heads), grid_spec=pltpu.P...]
  transfers between devices with their start and end apart: 4 -> 3, of which waited for: 4 -> 3; matrix products, arithmetic and copies ran while one was open for 3% -> 3% of each run, Pallas kernels for 30% -> 30%
where the time goes in v3:
time: 226 us; the launch traced here: 225 us
  Pallas kernels  149 us (66%)
  starting transfers between devices  34.2 us (15%)
  waiting for transfers between devices  31.8 us (14%)
  local copies, waits for them, and re-layouts  6.47 us (3%)
  other arithmetic  3.91 us (2%)
    pallas_call x1, Pallas kernels, deliver(): pl.pallas_call(functools.partial(deliver_kernel, group), grid=(rows,), in...  72.7 us
    pallas_call x2, Pallas kernels, attend(): pl.pallas_call(functools.partial(attend_kernel, heads), grid_spec=pltpu.P...  62.8 us
    all_to_all x3, starting transfers between devices, exchange(): return lax.all_to_all(block, 'seq', split_axis=0, concat_axis=0, tiled=True)  34.2 us
    all_to_all x3, waiting for transfers between devices, exchange(): return lax.all_to_all(block, 'seq', split_axis=0, concat_axis=0, tiled=True)  31.8 us
    pallas_call x2, Pallas kernels, unpack(): pl.pallas_call(unpack_kernel, grid=(rows,), in_specs=in_specs, out_specs=...  7.27 us
    pallas_call x1, Pallas kernels, pack(): pl.pallas_call(functools.partial(pack_kernel, rows), grid=(rows + 1 if wi...  6.22 us
  transfers between devices with their start and end apart: 3, of which 3 were waited for; matrix products, arithmetic and copies ran while one was open for 3% of the time, Pallas kernels for 30%

profile of v3, /device:TPU:0, one launch (start us, length us, event | category | flops | bytes accessed | tf_op | source)
XLA Modules:
  0.0 225.4 jit_solution(7825158392570769889)
XLA Ops:
  0.0 0.7 convert.7
  0.7 0.7 convert.8
  1.4 0.6 pad_maximum_fusion.ids_ref
  2.0 6.2 %shard_map.55.x_ref = bf16[8,976,256]{2,1,0:T(8,128)(2,1)} custom-call(bf16[8,256,512]{2,1,0:T(8,128)(2,1)} %q_ref.3, bf16[8,256,512]{2,1,0:T(8,128)(2,1)} %k_ref.3, bf16[8,256,512]{2,1,0:T(8,128)(2,1)} %v_ref.3, bf16[16,256]{1,0:T(8,128)(2,1)} %pad_maximum_fusion.ids_ref), custom_call_target="tpu_custom_call" | custom-call | flops 2621440 | bytes 7864320 | tf_op jit(solution)/shard_map/pallas_call | solution.py:36
  8.2 72.7 %shard_map.56 = (bf16[8,976,256]{2,1,0:T(8,128)(2,1)}, bf16[8,576,256]{2,1,0:T(8,128)(2,1)}) custom-call(bf16[8,976,256]{2,1,0:T(8,128)(2,1)} %shard_map.55.x_ref, bf16[8,256,512]{2,1,0:T(8,128)(2,1)} %q_ref.3, bf16[8,256,512]{2,1,0:T(8,128)(2,1)} %k_ref.3, bf16[8,256,512]{2,1,0:T(8,128)(2,1)} %v_ref.3), custom_call_target="tpu_custom_call" | custom-call | tf_op jit(solution)/shard_map/pallas_call | solution.py:95
  80.9 26.9 %all-to-all-start = ((bf16[8,576,256]{2,1,0:T(8,128)(2,1)}), bf16[8,576,256]{2,1,0:T(8,128)(2,1)S(1)}, u32[]{:S(2)}, u32[]{:S(2)}) async-start(bf16[8,576,256]{2,1,0:T(8,128)(2,1)} %get-tuple-element.8), calls=%async_computation | async-start | bytes 4718592 | tf_op jit(solution)/shard_map/all_to_all | solution.py:259
  107.9 0.9 convert_bitcast_fusion
  108.7 0.1 fusion.7
  108.8 0.1 copy.14
  109.0 0.1 copy.13
  109.1 0.7 broadcast_in_dim.17.enc_ref
  109.8 0.7 broadcast_in_dim.16.dec_ref
  110.5 0.4 convert_reduce_fusion.1
  110.9 0.6 subtract_minimum_fusion
  111.5 38.4 %shard_map.58 = bf16[8,5,64,256]{3,2,1,0:T(8,128)(2,1)} custom-call(s32[5,8]{1,0:T(8,128)} %bitcast.11, s32[5,8]{1,0:T(8,128)} %bitcast.10, bf16[8,976,256]{2,1,0:T(8,128)(2,1)} %get-tuple-element.7.x_ref, s32[5,1,2048]{2,1,0:T(1,128)} %broadcast_in_dim.16.dec_ref, s32[5,1,2048]{2,1,0:T(1,128)} %broadcast_in_dim.17.enc_ref), custom_call_target="tpu_custom_call" | custom-call | flops 2684354560 | bytes 5242880 | tf_op jit(solution)/shard_map/pallas_call | solution.py:224
  149.9 0.0 copy-start.4
  149.9 0.0 copy-start.3
  149.9 11.0 %all-to-all-done.x_ref = bf16[8,576,256]{2,1,0:T(8,128)(2,1)S(1)} async-done(((bf16[8,576,256]{2,1,0:T(8,128)(2,1)}), bf16[8,576,256]{2,1,0:T(8,128)(2,1)S(1)}, u32[]{:S(2)}, u32[]{:S(2)}) %all-to-all-start) | async-done | bytes 2359328 | tf_op jit(solution)/shard_map/all_to_all | solution.py:259
  160.9 0.0 copy-start.2
  160.9 1.4 copy-done.2
  162.3 3.6 %all-to-all-start.2 = ((bf16[8,5,64,256]{3,2,1,0:T(8,128)(2,1)}), bf16[8,5,64,256]{3,2,1,0:T(8,128)(2,1)S(1)}, u32[]{:S(2)}, u32[]{:S(2)}) async-start(bf16[8,5,64,256]{3,2,1,0:T(8,128)(2,1)} %shard_map.58), calls=%async_computation.2 | async-start | bytes 2621440 | tf_op jit(solution)/shard_map/all_to_all | solution.py:259
  165.9 0.0 copy-done.4
  165.9 0.6 slice.53.low_ref
  166.5 0.0 copy-done.3
  166.5 0.6 slice.54.high_ref
  167.1 0.6 broadcast_in_dim.15.enc_ref
  167.8 0.6 broadcast_in_dim.14.dec_ref
  168.4 24.4 %shard_map.57 = bf16[8,3,64,256]{3,2,1,0:T(8,128)(2,1)} custom-call(s32[3,8]{1,0:T(4,128)} %slice.53.low_ref, s32[3,8]{1,0:T(4,128)} %slice.54.high_ref, bf16[8,576,256]{2,1,0:T(8,128)(2,1)} %copy-done.2, s32[3,1,2048]{2,1,0:T(1,128)} %broadcast_in_dim.14.dec_ref, s32[3,1,2048]{2,1,0:T(1,128)} %broadcast_in_dim.15.enc_ref), custom_call_target="tpu_custom_call" | custom-call | flops 1610612736 | bytes 3145728 | tf_op jit(solution)/shard_map/pallas_call | solution.py:224
  192.8 4.7 %all-to-all-done.2.x_ref = bf16[8,5,64,256]{3,2,1,0:T(8,128)(2,1)S(1)} async-done(((bf16[8,5,64,256]{3,2,1,0:T(8,128)(2,1)}), bf16[8,5,64,256]{3,2,1,0:T(8,128)(2,1)S(1)}, u32[]{:S(2)}, u32[]{:S(2)}) %all-to-all-start.2) | async-done | bytes 1310752 | tf_op jit(solution)/shard_map/all_to_all | solution.py:259
  197.5 0.0 copy-start
  197.5 3.6 %all-to-all-start.1 = ((bf16[8,3,64,256]{3,2,1,0:T(8,128)(2,1)}), bf16[8,3,64,256]{3,2,1,0:T(8,128)(2,1)S(1)}, u32[]{:S(2)}, u32[]{:S(2)}) async-start(bf16[8,3,64,256]{3,2,1,0:T(8,128)(2,1)} %shard_map.57), calls=%async_computation.1 | async-start | bytes 1572864 | tf_op jit(solution)/shard_map/all_to_all | solution.py:259
  201.1 0.0 copy-done
  201.1 4.2 %shard_map.59.rest_0_ = bf16[8,256,512]{2,1,0:T(8,128)(2,1)} custom-call(bf16[8,5,64,256]{3,2,1,0:T(8,128)(2,1)} %copy-done), custom_call_target="tpu_custom_call" | custom-call | flops 2621440 | bytes 2621440 | tf_op jit(solution)/shard_map/pallas_call | solution.py:129
  205.4 16.1 %all-to-all-done.1.x_ref = bf16[8,3,64,256]{3,2,1,0:T(8,128)(2,1)S(1)} async-done(((bf16[8,3,64,256]{3,2,1,0:T(8,128)(2,1)}), bf16[8,3,64,256]{3,2,1,0:T(8,128)(2,1)S(1)}, u32[]{:S(2)}, u32[]{:S(2)}) %all-to-all-start.1) | async-done | bytes 786464 | tf_op jit(solution)/shard_map/all_to_all | solution.py:259
  221.5 0.0 copy-start.1
  221.5 0.9 copy-done.1
  222.4 3.0 %shard_map.60 = bf16[8,256,512]{2,1,0:T(8,128)(2,1)} custom-call(bf16[8,3,64,256]{3,2,1,0:T(8,128)(2,1)} %copy-done.1, bf16[8,256,512]{2,1,0:T(8,128)(2,1)} %shard_map.59.rest_0_), custom_call_target="tpu_custom_call", output_to_operand_aliasing={{}: (1, {})} | custom-call | flops 1572864 | bytes 1572864 | tf_op jit(solution)/shard_map/pallas_call | solution.py:129
  (7 shorter events, 0.1 us)
Async XLA Ops:
  80.9 79.9 %all-to-all-start = ((bf16[8,576,256]{2,1,0:T(8,128)(2,1)}), bf16[8,576,256]{2,1,0:T(8,128)(2,1)S(1)}, u32[]{:S(2)}, u32[]{:S(2)}) async-start(bf16[8,576,256]{2,1,0:T(8,128)(2,1)} %get-tuple-element.8), calls=%async_computation | async-start | bytes 4718592 | tf_op jit(solution)/shard_map/all_to_all | solution.py:259
  149.9 16.0 %copy-start.4 = (s32[8,8]{1,0:T(8,128)S(1)}, s32[8,8]{1,0:T(8,128)}, u32[]{:S(2)}) copy-start(s32[8,8]{1,0:T(8,128)} %get-tuple-element.11) | copy-start | bytes 772
  149.9 16.6 %copy-start.3 = (s32[8,8]{1,0:T(8,128)S(1)}, s32[8,8]{1,0:T(8,128)}, u32[]{:S(2)}) copy-start(s32[8,8]{1,0:T(8,128)} %get-tuple-element.12) | copy-start | bytes 772
  160.9 1.4 copy-start.2
  162.3 35.2 %all-to-all-start.2 = ((bf16[8,5,64,256]{3,2,1,0:T(8,128)(2,1)}), bf16[8,5,64,256]{3,2,1,0:T(8,128)(2,1)S(1)}, u32[]{:S(2)}, u32[]{:S(2)}) async-start(bf16[8,5,64,256]{3,2,1,0:T(8,128)(2,1)} %shard_map.58), calls=%async_computation.2 | async-start | bytes 2621440 | tf_op jit(solution)/shard_map/all_to_all | solution.py:259
  197.5 3.6 %copy-start = (bf16[8,5,64,256]{3,2,1,0:T(8,128)(2,1)}, bf16[8,5,64,256]{3,2,1,0:T(8,128)(2,1)S(1)}, u32[]{:S(2)}) copy-start(bf16[8,5,64,256]{3,2,1,0:T(8,128)(2,1)S(1)} %all-to-all-done.2.x_ref) | copy-start | bytes 3932164
  197.5 24.0 %all-to-all-start.1 = ((bf16[8,3,64,256]{3,2,1,0:T(8,128)(2,1)}), bf16[8,3,64,256]{3,2,1,0:T(8,128)(2,1)S(1)}, u32[]{:S(2)}, u32[]{:S(2)}) async-start(bf16[8,3,64,256]{3,2,1,0:T(8,128)(2,1)} %shard_map.57), calls=%async_computation.1 | async-start | bytes 1572864 | tf_op jit(solution)/shard_map/all_to_all | solution.py:259
  221.5 0.9 copy-start.1

commit v4 on v3

--- a/solution.py
+++ b/solution.py
@@ -67,7 +67,7 @@
                 barrier, inc=1, device_id={"seq": lax.rem(me + shift, group)}, device_id_type=pl.DeviceIdType.MESH
             )
         pl.semaphore_wait(barrier, group - 1)
-        for shift in range(1, group):
+        for shift in sorted(range(1, group), key=lambda shift: abs(2 * shift - group)):
             transfer(shift).start()
         own = pltpu.make_async_copy(x_ref.at[me], held, own_sem)
         own.start()

time: 226 us -> 226 us (level)
  starting transfers between devices: 34.2 us -> 29.5 us
    all_to_all x3, starting transfers between devices: 34.2 us -> 29.5 us  [exchange(): return lax.all_to_all(block, 'seq', split_axis=0, concat_axis=0, tiled=True)]
    pallas_call x1, Pallas kernels: 72.7 us -> 75.7 us  [deliver(): pl.pallas_call(functools.partial(deliver_kernel, group), grid=(rows,), in...]
  transfers between devices with their start and end apart: 3 -> 3, of which waited for: 3 -> 3; matrix products, arithmetic and copies ran while one was open for 3% -> 3% of each run, Pallas kernels for 30% -> 29%
where the time goes in v4:
time: 226 us; the launch traced here: 225 us
  Pallas kernels  151 us (67%)
  waiting for transfers between devices  33.6 us (15%)
  starting transfers between devices  29.5 us (13%)
  local copies, waits for them, and re-layouts  6.47 us (3%)
  other arithmetic  3.91 us (2%)
    pallas_call x1, Pallas kernels, deliver(): pl.pallas_call(functools.partial(deliver_kernel, group), grid=(rows,), in...  75.7 us
    pallas_call x2, Pallas kernels, attend(): pl.pallas_call(functools.partial(attend_kernel, heads), grid_spec=pltpu.P...  62 us
    all_to_all x3, waiting for transfers between devices, exchange(): return lax.all_to_all(block, 'seq', split_axis=0, concat_axis=0, tiled=True)  33.6 us
    all_to_all x3, starting transfers between devices, exchange(): return lax.all_to_all(block, 'seq', split_axis=0, concat_axis=0, tiled=True)  29.5 us
    pallas_call x2, Pallas kernels, unpack(): pl.pallas_call(unpack_kernel, grid=(rows,), in_specs=in_specs, out_specs=...  7.27 us
    pallas_call x1, Pallas kernels, pack(): pl.pallas_call(functools.partial(pack_kernel, rows), grid=(rows + 1 if wi...  6.22 us
  transfers between devices with their start and end apart: 3, of which 3 were waited for; matrix products, arithmetic and copies ran while one was open for 3% of the time, Pallas kernels for 29%

profile of v4, /device:TPU:0, one launch (start us, length us, event | category | flops | bytes accessed | tf_op | source)
XLA Modules:
  0.0 224.7 jit_solution(6140431782022257395)
XLA Ops:
  0.0 0.7 convert.7
  0.7 0.7 convert.8
  1.4 0.6 pad_maximum_fusion.ids_ref
  2.0 6.2 %shard_map.55.x_ref = bf16[8,976,256]{2,1,0:T(8,128)(2,1)} custom-call(bf16[8,256,512]{2,1,0:T(8,128)(2,1)} %q_ref.3, bf16[8,256,512]{2,1,0:T(8,128)(2,1)} %k_ref.3, bf16[8,256,512]{2,1,0:T(8,128)(2,1)} %v_ref.3, bf16[16,256]{1,0:T(8,128)(2,1)} %pad_maximum_fusion.ids_ref), custom_call_target="tpu_custom_call" | custom-call | flops 2621440 | bytes 7864320 | tf_op jit(solution)/shard_map/pallas_call | solution.py:36
  8.2 75.7 %shard_map.56 = (bf16[8,976,256]{2,1,0:T(8,128)(2,1)}, bf16[8,576,256]{2,1,0:T(8,128)(2,1)}) custom-call(bf16[8,976,256]{2,1,0:T(8,128)(2,1)} %shard_map.55.x_ref, bf16[8,256,512]{2,1,0:T(8,128)(2,1)} %q_ref.3, bf16[8,256,512]{2,1,0:T(8,128)(2,1)} %k_ref.3, bf16[8,256,512]{2,1,0:T(8,128)(2,1)} %v_ref.3), custom_call_target="tpu_custom_call" | custom-call | tf_op jit(solution)/shard_map/pallas_call | solution.py:95
  83.9 22.2 %all-to-all-start = ((bf16[8,576,256]{2,1,0:T(8,128)(2,1)}), bf16[8,576,256]{2,1,0:T(8,128)(2,1)S(1)}, u32[]{:S(2)}, u32[]{:S(2)}) async-start(bf16[8,576,256]{2,1,0:T(8,128)(2,1)} %get-tuple-element.8), calls=%async_computation | async-start | bytes 4718592 | tf_op jit(solution)/shard_map/all_to_all | solution.py:259
  106.1 0.9 convert_bitcast_fusion
  107.0 0.1 fusion.7
  107.1 0.1 copy.14
  107.2 0.1 copy.13
  107.4 0.7 broadcast_in_dim.17.enc_ref
  108.0 0.7 broadcast_in_dim.16.dec_ref
  108.7 0.4 convert_reduce_fusion.1
  109.1 0.6 subtract_minimum_fusion
  109.8 39.6 %shard_map.58 = bf16[8,5,64,256]{3,2,1,0:T(8,128)(2,1)} custom-call(s32[5,8]{1,0:T(8,128)} %bitcast.11, s32[5,8]{1,0:T(8,128)} %bitcast.10, bf16[8,976,256]{2,1,0:T(8,128)(2,1)} %get-tuple-element.7.x_ref, s32[5,1,2048]{2,1,0:T(1,128)} %broadcast_in_dim.16.dec_ref, s32[5,1,2048]{2,1,0:T(1,128)} %broadcast_in_dim.17.enc_ref), custom_call_target="tpu_custom_call" | custom-call | flops 2684354560 | bytes 5242880 | tf_op jit(solution)/shard_map/pallas_call | solution.py:224
  149.3 0.0 copy-start.4
  149.3 0.0 copy-start.3
  149.3 10.8 %all-to-all-done.x_ref = bf16[8,576,256]{2,1,0:T(8,128)(2,1)S(1)} async-done(((bf16[8,576,256]{2,1,0:T(8,128)(2,1)}), bf16[8,576,256]{2,1,0:T(8,128)(2,1)S(1)}, u32[]{:S(2)}, u32[]{:S(2)}) %all-to-all-start) | async-done | bytes 2359328 | tf_op jit(solution)/shard_map/all_to_all | solution.py:259
  160.1 0.0 copy-start.2
  160.1 1.4 copy-done.2
  161.6 3.6 %all-to-all-start.2 = ((bf16[8,5,64,256]{3,2,1,0:T(8,128)(2,1)}), bf16[8,5,64,256]{3,2,1,0:T(8,128)(2,1)S(1)}, u32[]{:S(2)}, u32[]{:S(2)}) async-start(bf16[8,5,64,256]{3,2,1,0:T(8,128)(2,1)} %shard_map.58), calls=%async_computation.2 | async-start | bytes 2621440 | tf_op jit(solution)/shard_map/all_to_all | solution.py:259
  165.2 0.0 copy-done.4
  165.2 0.6 slice.53.low_ref
  165.8 0.0 copy-done.3
  165.8 0.6 slice.54.high_ref
  166.4 0.6 broadcast_in_dim.15.enc_ref
  167.1 0.6 broadcast_in_dim.14.dec_ref
  167.7 22.4 %shard_map.57 = bf16[8,3,64,256]{3,2,1,0:T(8,128)(2,1)} custom-call(s32[3,8]{1,0:T(4,128)} %slice.53.low_ref, s32[3,8]{1,0:T(4,128)} %slice.54.high_ref, bf16[8,576,256]{2,1,0:T(8,128)(2,1)} %copy-done.2, s32[3,1,2048]{2,1,0:T(1,128)} %broadcast_in_dim.14.dec_ref, s32[3,1,2048]{2,1,0:T(1,128)} %broadcast_in_dim.15.enc_ref), custom_call_target="tpu_custom_call" | custom-call | flops 1610612736 | bytes 3145728 | tf_op jit(solution)/shard_map/pallas_call | solution.py:224
  190.1 6.6 %all-to-all-done.2.x_ref = bf16[8,5,64,256]{3,2,1,0:T(8,128)(2,1)S(1)} async-done(((bf16[8,5,64,256]{3,2,1,0:T(8,128)(2,1)}), bf16[8,5,64,256]{3,2,1,0:T(8,128)(2,1)S(1)}, u32[]{:S(2)}, u32[]{:S(2)}) %all-to-all-start.2) | async-done | bytes 1310752 | tf_op jit(solution)/shard_map/all_to_all | solution.py:259
  196.8 0.0 copy-start
  196.8 3.6 %all-to-all-start.1 = ((bf16[8,3,64,256]{3,2,1,0:T(8,128)(2,1)}), bf16[8,3,64,256]{3,2,1,0:T(8,128)(2,1)S(1)}, u32[]{:S(2)}, u32[]{:S(2)}) async-start(bf16[8,3,64,256]{3,2,1,0:T(8,128)(2,1)} %shard_map.57), calls=%async_computation.1 | async-start | bytes 1572864 | tf_op jit(solution)/shard_map/all_to_all | solution.py:259
  200.4 0.0 copy-done
  200.4 4.2 %shard_map.59.rest_0_ = bf16[8,256,512]{2,1,0:T(8,128)(2,1)} custom-call(bf16[8,5,64,256]{3,2,1,0:T(8,128)(2,1)} %copy-done), custom_call_target="tpu_custom_call" | custom-call | flops 2621440 | bytes 2621440 | tf_op jit(solution)/shard_map/pallas_call | solution.py:129
  204.6 16.1 %all-to-all-done.1.x_ref = bf16[8,3,64,256]{3,2,1,0:T(8,128)(2,1)S(1)} async-done(((bf16[8,3,64,256]{3,2,1,0:T(8,128)(2,1)}), bf16[8,3,64,256]{3,2,1,0:T(8,128)(2,1)S(1)}, u32[]{:S(2)}, u32[]{:S(2)}) %all-to-all-start.1) | async-done | bytes 786464 | tf_op jit(solution)/shard_map/all_to_all | solution.py:259
  220.8 0.0 copy-start.1
  220.8 0.9 copy-done.1
  221.7 3.0 %shard_map.60 = bf16[8,256,512]{2,1,0:T(8,128)(2,1)} custom-call(bf16[8,3,64,256]{3,2,1,0:T(8,128)(2,1)} %copy-done.1, bf16[8,256,512]{2,1,0:T(8,128)(2,1)} %shard_map.59.rest_0_), custom_call_target="tpu_custom_call", output_to_operand_aliasing={{}: (1, {})} | custom-call | flops 1572864 | bytes 1572864 | tf_op jit(solution)/shard_map/pallas_call | solution.py:129
  (7 shorter events, 0.1 us)
Async XLA Ops:
  83.9 76.2 %all-to-all-start = ((bf16[8,576,256]{2,1,0:T(8,128)(2,1)}), bf16[8,576,256]{2,1,0:T(8,128)(2,1)S(1)}, u32[]{:S(2)}, u32[]{:S(2)}) async-start(bf16[8,576,256]{2,1,0:T(8,128)(2,1)} %get-tuple-element.8), calls=%async_computation | async-start | bytes 4718592 | tf_op jit(solution)/shard_map/all_to_all | solution.py:259
  149.3 15.8 %copy-start.4 = (s32[8,8]{1,0:T(8,128)S(1)}, s32[8,8]{1,0:T(8,128)}, u32[]{:S(2)}) copy-start(s32[8,8]{1,0:T(8,128)} %get-tuple-element.11) | copy-start | bytes 772
  149.3 16.4 %copy-start.3 = (s32[8,8]{1,0:T(8,128)S(1)}, s32[8,8]{1,0:T(8,128)}, u32[]{:S(2)}) copy-start(s32[8,8]{1,0:T(8,128)} %get-tuple-element.12) | copy-start | bytes 772
  160.1 1.4 copy-start.2
  161.6 35.2 %all-to-all-start.2 = ((bf16[8,5,64,256]{3,2,1,0:T(8,128)(2,1)}), bf16[8,5,64,256]{3,2,1,0:T(8,128)(2,1)S(1)}, u32[]{:S(2)}, u32[]{:S(2)}) async-start(bf16[8,5,64,256]{3,2,1,0:T(8,128)(2,1)} %shard_map.58), calls=%async_computation.2 | async-start | bytes 2621440 | tf_op jit(solution)/shard_map/all_to_all | solution.py:259
  196.8 3.6 %copy-start = (bf16[8,5,64,256]{3,2,1,0:T(8,128)(2,1)}, bf16[8,5,64,256]{3,2,1,0:T(8,128)(2,1)S(1)}, u32[]{:S(2)}) copy-start(bf16[8,5,64,256]{3,2,1,0:T(8,128)(2,1)S(1)} %all-to-all-done.2.x_ref) | copy-start | bytes 3932164
  196.8 24.0 %all-to-all-start.1 = ((bf16[8,3,64,256]{3,2,1,0:T(8,128)(2,1)}), bf16[8,3,64,256]{3,2,1,0:T(8,128)(2,1)S(1)}, u32[]{:S(2)}, u32[]{:S(2)}) async-start(bf16[8,3,64,256]{3,2,1,0:T(8,128)(2,1)} %shard_map.57), calls=%async_computation.1 | async-start | bytes 1572864 | tf_op jit(solution)/shard_map/all_to_all | solution.py:259
  220.8 0.9 copy-start.1
